TPU v7x, 128 devices: a whole 4x4x4 slice. The times are simulated.
128 devices in a mesh: dp: 16 (over y, x), expert: 4 (over z), tensor: 2 (over core).
Axes of the slice: x: 4, y: 4, z: 4, core: 2. Of those that a mesh axis runs over, the one named last changes fastest.
Arguments:
- tokens: bfloat16 [8192, 2048], P(('dp', 'expert'), 'tensor'), may hold values from -6 to 6
- norm_gain: bfloat16 [2048], replicated, may hold values from 0.25 to 1.75
- expert_ids: int32 [8192, 2], P(('dp', 'expert')), may hold values from 0 to 3, all different within a row; in each aligned block of 128 rows (0 to 127, 128 to 255, ...) at most 128 rows name the same one
- gate_codes: int32 [8192, 2], P(('dp', 'expert')), may hold values from 1 to 255
- gate_weights: bfloat16 [4, 7168, 2048], P('expert', ('dp', 'tensor')), may hold values from -0.125 to 0.125
- up_weights: bfloat16 [4, 7168, 2048], P('expert', ('dp', 'tensor')), may hold values from -0.125 to 0.125
- down_weights: bfloat16 [4, 7168, 2048], P('expert', ('dp', 'tensor')), may hold values from -0.0625 to 0.0625
- value_head: bfloat16 [2048, 128], replicated, may hold values from -0.125 to 0.125
- actions: int32 [8192], P(('dp', 'expert')), may hold values from 0 to 127
- rewards: int32 [8192], P(('dp', 'expert')), may hold values from -8 to 8
- trace_codes: int32 [8192], P(('dp', 'expert')), may hold values from 1 to 1024
Outputs:
- action_values: float32 [8192, 128], P(('dp', 'expert'))
- retrace_targets: float32 [8192], P(('dp', 'expert'))
Inputs may be any that keep to these rules, and one draw needn't show every extreme that they name: `expert_ids`: each row names 2 different experts; within the 128 rows of one index pair of dp and expert each expert is named by at most 128 rows, and in some of these blocks one expert by exactly 128.
All inputs are finite; a program needn't handle non-finite values.
Results may differ from a plain program's by a relative error of at most 0.005.
Values may be sent and summed in bfloat16 or wider, within the bound.
A program may use at most 256 MiB of HBM per device.

v0:
```python
import jax
import jax.numpy as jnp
from jax import lax
from jax.sharding import PartitionSpec as P

TOP = 2
STEPS = 128


DISCOUNT = 0.99
EPSILON = 1e-05


def joined_along(tiles, dim):
    tiles = jnp.moveaxis(tiles, 0, dim)
    shape = tiles.shape
    return tiles.reshape(*shape[:dim], shape[dim] * shape[dim + 1], *shape[dim + 2 :])


def copy_for_each(value, axis):
    size = lax.axis_size(axis)
    return lax.all_to_all(
        jnp.broadcast_to(value[None], (size, *value.shape)), axis, 0, 0, tiled=True
    )


def gathered_copies(value, axis, dim):
    return joined_along(copy_for_each(value, axis), dim)


def side_by_side(arrays, axis, dim, along):
    both = jnp.concatenate(arrays, axis=along)
    whole, at, finished = (lax.all_gather(both, axis, axis=dim, tiled=True), 0, [])
    for a in arrays:
        finished.append(lax.slice_in_dim(whole, at, at + a.shape[along], axis=along))
        at += a.shape[along]
    return tuple(finished)


def taken_together(value, axis):
    return copy_for_each(value, axis).sum(axis=0)


def expert_rows(row_block, gate_matrix, lift_matrix, down_matrix):
    gate_value = lax.dot_general(
        row_block, gate_matrix, (((1,), (1,)), ((), ())), preferred_element_type=jnp.float32
    )
    lift_value = lax.dot_general(
        row_block, lift_matrix, (((1,), (1,)), ((), ())), preferred_element_type=jnp.float32
    )
    hidden = (jax.nn.silu(gate_value) * lift_value).astype(jnp.bfloat16)
    return jnp.dot(hidden, down_matrix, preferred_element_type=jnp.float32)


def retrace(action_values, actions, rewards, trace_codes):
    greedy = jnp.max(action_values, axis=1)
    picked = (
        actions[:, None] == jnp.arange(action_values.shape[1], dtype=jnp.int32)[None, :]
    ).astype(jnp.float32)
    taken = jnp.sum(action_values * picked, axis=1)
    trace = trace_codes.astype(jnp.float32) / 1024.0
    reward = rewards.astype(jnp.float32) * 0.25
    greedy = greedy.reshape(-1, STEPS)
    taken = taken.reshape(-1, STEPS)
    trace = trace.reshape(-1, STEPS)
    reward = reward.reshape(-1, STEPS)
    padding = jnp.zeros_like(greedy[:, :1])
    greedy_next = jnp.concatenate([greedy[:, 1:], padding], axis=1)
    taken_next = jnp.concatenate([taken[:, 1:], padding], axis=1)
    trace_next = jnp.concatenate([trace[:, 1:], padding], axis=1)
    driver = reward + DISCOUNT * (greedy_next - trace_next * taken_next)
    log_sums = jnp.cumsum(jnp.log(DISCOUNT * trace), axis=1)
    spans = log_sums[:, None, :] - log_sums[:, :, None]
    upper_mask = (
        jnp.arange(STEPS, dtype=jnp.int32)[None, :] >= jnp.arange(STEPS, dtype=jnp.int32)[:, None]
    )
    weight = jnp.where(upper_mask[None, :, :], jnp.exp(jnp.minimum(spans, 0.0)), 0.0)
    target = jnp.einsum("nts,ns->nt", weight, driver, precision=lax.Precision.HIGHEST)
    return target.reshape(-1)


def per_device(
    tokens,
    norm_gain,
    expert_ids,
    gate_codes,
    gate_weights,
    up_weights,
    down_weights,
    value_head,
    actions,
    rewards,
    trace_codes,
):
    groups = lax.axis_size("expert")
    tok_rows = tokens.shape[0]
    capacity = 2 * tok_rows * TOP // groups
    head_wide = value_head.astype(jnp.float32)
    flat_ids = expert_ids.reshape(-1)
    marked = (flat_ids[:, None] == jnp.arange(groups, dtype=jnp.int32)[None, :]).astype(jnp.int32)
    places = jnp.sum((jnp.cumsum(marked, axis=0) - 1) * marked, axis=1)
    slot_of = (flat_ids * capacity + places).reshape(tok_rows, TOP)
    slot_range = jnp.arange(groups * capacity, dtype=jnp.int32)
    matches = slot_of[None, :, :] == slot_range[:, None, None]
    dispatch_map = jnp.any(matches, axis=2).astype(jnp.bfloat16)
    outgoing = jnp.dot(dispatch_map, tokens, preferred_element_type=jnp.float32).astype(
        jnp.bfloat16
    )
    outgoing = outgoing.reshape(groups, capacity, tokens.shape[1])
    arrived = lax.all_to_all(outgoing, "expert", split_axis=0, concat_axis=0, tiled=True)
    arrived = gathered_copies(arrived, "tensor", 2)
    row_count = groups * capacity
    row_block = arrived.reshape(row_count, arrived.shape[2])
    widened = row_block.astype(jnp.float32)
    scaling = lax.rsqrt(jnp.mean(widened * widened, axis=1, keepdims=True) + EPSILON)
    normed = (widened * scaling * norm_gain.astype(jnp.float32)[None, :]).astype(jnp.bfloat16)
    pieces = side_by_side((gate_weights, up_weights, down_weights), "dp", 1, 0)
    partial_value = expert_rows(normed, pieces[0][0], pieces[1][0], pieces[2][0])
    payload = jnp.dot(
        partial_value,
        head_wide,
        precision=lax.Precision.HIGHEST,
        preferred_element_type=jnp.float32,
    )
    returned = lax.all_to_all(
        payload.reshape(groups, capacity, payload.shape[1]).astype(jnp.bfloat16),
        "expert",
        split_axis=0,
        concat_axis=0,
        tiled=True,
    ).astype(jnp.float32)
    returned = returned.reshape(row_count, payload.shape[1])
    codes = gate_codes.astype(jnp.float32)
    gate_share = codes / jnp.sum(codes, axis=1, keepdims=True)
    combine_map = jnp.sum(jnp.where(matches, gate_share[None, :, :], 0.0), axis=2)
    blended = lax.dot_general(
        combine_map,
        returned,
        (((0,), (0,)), ((), ())),
        precision=lax.Precision.HIGHEST,
        preferred_element_type=jnp.float32,
    )
    action_values = taken_together(blended, "tensor")
    retrace_targets = retrace(action_values, actions, rewards, trace_codes)
    return (action_values, retrace_targets)


def solution(mesh):
    in_specs = (
        P(("dp", "expert"), "tensor"),
        P(),
        P(("dp", "expert"), None),
        P(("dp", "expert"), None),
        P("expert", ("dp", "tensor"), None),
        P("expert", ("dp", "tensor"), None),
        P("expert", ("dp", "tensor"), None),
        P(),
        P(("dp", "expert")),
        P(("dp", "expert")),
        P(("dp", "expert")),
    )
    out_specs = (P(("dp", "expert"), None), P(("dp", "expert")))
    return jax.shard_map(
        per_device, mesh=mesh, in_specs=in_specs, out_specs=out_specs, check_vma=False
    )
```

profile of v0, /device:TPU:1, one launch (start us, length us, event | category | flops | bytes accessed | tf_op | source)
XLA Modules:
  0.0 327.6 jit_solution(11318493623781641694)
XLA Ops:
  7.2 3.6 %pad_maximum_fusion = bf16[3,224,2048]{2,1,0:T(8,128)(2,1)} fusion(bf16[1,224,2048]{2,1,0:T(8,128)(2,1)} %param.17, bf16[1,224,2048]{2,1,0:T(8,128)(2,1)} %param.16, bf16[1,224,2048]{2,1,0:T(8,128)(2,1)} %param.15), kind=kLoop, calls=%fused_computation.12 | loop fusion | flops 2752512 | bytes 5505024 | tf_op jit(solution)/shard_map/concatenate | solution.py:32
  10.9 0.1 copy.44
  11.0 0.1 eq.53
  11.2 0.1 eq.49
  11.3 1.2 reduce-window.14
  12.6 0.1 copy.46
  12.8 0.1 copy.47
  13.0 0.1 reduce_sum.57
  13.2 0.1 fusion.7
  13.3 1.4 convolution_convert_fusion
  14.7 5.8 %all-to-all-start = ((bf16[4,128,1024]{2,1,0:T(8,128)(2,1)}), bf16[4,128,1024]{2,1,0:T(8,128)(2,1)S(1)}, u32[]{:S(2)}, u32[]{:S(2)}) async-start(bf16[4,128,1024]{2,1,0:T(8,128)(2,1)} %bitcast.2), calls=%async_computation | async-start | bytes 2097152 | tf_op jit(solution)/shard_map/all_to_all | solution.py:110
  20.6 0.1 copy.50
  20.7 0.2 reduce-window.19
  20.9 0.1 reduce.2
  21.1 13.7 %all-to-all-done = bf16[4,128,1024]{2,1,0:T(8,128)(2,1)S(1)} async-done(((bf16[4,128,1024]{2,1,0:T(8,128)(2,1)}), bf16[4,128,1024]{2,1,0:T(8,128)(2,1)S(1)}, u32[]{:S(2)}, u32[]{:S(2)}) %all-to-all-start) | async-done | bytes 1048608 | tf_op jit(solution)/shard_map/all_to_all | solution.py:110
  34.8 0.3 broadcast_in_dim.19
  35.1 6.9 %all_to_all.20 = bf16[2,4,128,1024]{3,2,1,0:T(8,128)(2,1)S(1)} all-to-all(bf16[2,4,128,1024]{3,2,1,0:T(8,128)(2,1)S(1)} %broadcast_in_dim.19), channel_id=1, replica_groups=mesh['dp'=16,'expert'=4,'tensor'=2] {'tensor'}, dimensions={0} | all-to-all | bytes 4194304 | tf_op jit(solution)/shard_map/all_to_all | solution.py:22
  41.9 0.5 fusion.3
  42.4 0.5 fusion.6
  43.0 2.2 copy.49
  45.2 0.6 copy.52
  45.8 218.8 %all-gather.2.cloned.1.call-done = bf16[3,3584,2048]{2,1,0:T(8,128)(2,1)} async-done(((bf16[3,224,2048]{2,1,0:T(8,128)(2,1)}), bf16[3,3584,2048]{2,1,0:T(8,128)(2,1)}) %all-gather.2.cloned.1.call-update) | async-done | bytes 44040208 | tf_op jit(solution)/shard_map/all_gather | solution.py:33
  264.6 13.1 %fusion.2 = f32[512,3584]{1,0:T(8,128)} fusion(bf16[512,2048]{1,0:T(8,128)(2,1)S(1)} %bitcast.61, bf16[3,3584,2048]{2,1,0:T(8,128)(2,1)} %all-gather.2.cloned.1.call-done), kind=kOutput, calls=%fused_computation.5 | convolution fusion | flops 7516192768 | bytes 24117248 | tf_op jit(solution)/shard_map/dot_general | solution.py:45
  277.7 12.7 %multiply_convert_fusion = bf16[512,3584]{1,0:T(8,128)(2,1)S(1)} fusion(f32[512,3584]{1,0:T(8,128)} %fusion.2, bf16[512,2048]{1,0:T(8,128)(2,1)S(1)} %bitcast.62, bf16[3,3584,2048]{2,1,0:T(8,128)(2,1)} %all-gather.2.cloned.1.call-done), kind=kOutput, calls=%fused_computation.6 | convolution fusion | flops 7527202816 | bytes 27787264 | tf_op jit(solution)/shard_map/dot_general | solution.py:48
  290.4 11.5 %fusion = f32[512,2048]{1,0:T(8,128)S(1)} fusion(bf16[512,3584]{1,0:T(8,128)(2,1)S(1)} %multiply_convert_fusion, bf16[3,3584,2048]{2,1,0:T(8,128)(2,1)} %all-gather.2.cloned.1.call-done), kind=kOutput, calls=%fused_computation.1 | convolution fusion | flops 7516192768 | bytes 22544384 | tf_op jit(solution)/shard_map/dot_general | solution.py:52
  301.9 2.6 convolution_convert_fusion.1
  304.5 4.1 %all-to-all-start.2 = ((bf16[4,128,128]{2,1,0:T(8,128)(2,1)}), bf16[4,128,128]{2,1,0:T(8,128)(2,1)S(1)}, u32[]{:S(2)}, u32[]{:S(2)}) async-start(bf16[4,128,128]{2,1,0:T(8,128)(2,1)} %bitcast.7), calls=%async_computation.2 | async-start | bytes 262144 | tf_op jit(solution)/shard_map/all_to_all | solution.py:125
  308.7 4.8 %all-to-all-done.2 = bf16[4,128,128]{2,1,0:T(8,128)(2,1)S(1)} async-done(((bf16[4,128,128]{2,1,0:T(8,128)(2,1)}), bf16[4,128,128]{2,1,0:T(8,128)(2,1)S(1)}, u32[]{:S(2)}, u32[]{:S(2)}) %all-to-all-start.2) | async-done | bytes 131104 | tf_op jit(solution)/shard_map/all_to_all | solution.py:125
  313.4 0.4 fusion.31
  313.8 5.8 %all_to_all.21 = f32[2,128,128]{2,1,0:T(8,128)S(1)} all-to-all(f32[2,128,128]{2,1,0:T(8,128)S(1)} %broadcast_in_dim.20), channel_id=1, replica_groups=mesh['dp'=16,'expert'=4,'tensor'=2] {'tensor'}, dimensions={0} | all-to-all | bytes 262144 | tf_op jit(solution)/shard_map/all_to_all | solution.py:22
  319.6 0.2 select_reduce_fusion.1
  319.9 0.8 convolution_bitcast_fusion
  (38 shorter events, 0.7 us)
Async XLA Ops:
  7.2 294.7 %copy-start = (bf16[2048,128]{1,0:T(8,128)(2,1)S(1)}, bf16[2048,128]{1,0:T(8,128)(2,1)}, u32[]{:S(2)}) copy-start(bf16[2048,128]{1,0:T(8,128)(2,1)} %param.18) | copy-start | bytes 1572868
  7.2 3.7 %copy-start.3 = (s32[128,2]{0,1:T(2,128)S(1)}, s32[128,2]{0,1:T(2,128)}, u32[]{:S(2)}) copy-start(s32[128,2]{0,1:T(2,128)} %param.13) | copy-start | bytes 3076
  7.2 6.1 %copy-start.2 = (bf16[128,1024]{1,0:T(8,128)(2,1)S(1)}, bf16[128,1024]{1,0:T(8,128)(2,1)}, u32[]{:S(2)}) copy-start(bf16[128,1024]{1,0:T(8,128)(2,1)} %param.11) | copy-start | bytes 786436
  7.2 257.4 %all-gather.2.cloned.1.call-start = ((), (), s32[]{:S(2)}) async-start(), calls=%async_computation.4 | async-start | bytes 46792704 | tf_op jit(solution)/shard_map/all_gather | solution.py:33
  10.9 9.7 %copy-start.4 = (bf16[2048]{0:T(1024)(128)(2,1)S(1)}, bf16[2048]{0:T(1024)(128)(2,1)}, u32[]{:S(2)}) copy-start(bf16[2048]{0:T(1024)(128)(2,1)} %param.12) | copy-start | bytes 12292
  10.9 9.7 %copy-start.7 = (s32[128]{0:T(128)S(1)}, s32[128]{0:T(128)}, u32[]{:S(2)}) copy-start(s32[128]{0:T(128)} %param.21) | copy-start | bytes 1540
  10.9 10.1 %copy-start.5 = (s32[128,2]{0,1:T(2,128)S(1)}, s32[128,2]{0,1:T(2,128)}, u32[]{:S(2)}) copy-start(s32[128,2]{0,1:T(2,128)} %param.14) | copy-start | bytes 3076
  14.7 20.1 %all-to-all-start = ((bf16[4,128,1024]{2,1,0:T(8,128)(2,1)}), bf16[4,128,1024]{2,1,0:T(8,128)(2,1)S(1)}, u32[]{:S(2)}, u32[]{:S(2)}) async-start(bf16[4,128,1024]{2,1,0:T(8,128)(2,1)} %bitcast.2), calls=%async_computation | async-start | bytes 2097152 | tf_op jit(solution)/shard_map/all_to_all | solution.py:110
  301.8 17.8 %copy-start.6 = (s32[128]{0:T(128)S(1)}, s32[128]{0:T(128)}, u32[]{:S(2)}) copy-start(s32[128]{0:T(128)} %param.19) | copy-start | bytes 1540
  301.9 18.0 %copy-start.8 = (s32[128]{0:T(128)S(1)}, s32[128]{0:T(128)}, u32[]{:S(2)}) copy-start(s32[128]{0:T(128)} %param.20) | copy-start | bytes 1540
  304.5 9.0 %all-to-all-start.2 = ((bf16[4,128,128]{2,1,0:T(8,128)(2,1)}), bf16[4,128,128]{2,1,0:T(8,128)(2,1)S(1)}, u32[]{:S(2)}, u32[]{:S(2)}) async-start(bf16[4,128,128]{2,1,0:T(8,128)(2,1)} %bitcast.7), calls=%async_computation.2 | async-start | bytes 262144 | tf_op jit(solution)/shard_map/all_to_all | solution.py:125
  319.6 1.1 copy-start.1
Sparse Core Ops, SparseCore 0:
  11.0 253.4 all-gather.1
where the time goes:
time: 328 us
  waiting for transfers between devices  237 us (72%)
  matrix products  42.5 us (13%)
  between operations  14.2 us (4%)
  blocking collectives  12.6 us (4%)
  starting transfers between devices  10 us (3%)
  other arithmetic  6.68 us (2%)
  local copies, waits for them, and re-layouts  4.22 us (1%)
    all_gather x1, waiting for transfers between devices, side_by_side(): lax.all_gather(both, axis, axis=dim, tiled=True)  219 us
    all_to_all x1, waiting for transfers between devices, per_device(): lax.all_to_all(outgoing, 'expert', split_axis=0, concat_axis=0, tiled=True)  13.7 us
    dot_general x1, matrix products, expert_rows(): lax.dot_general(row_block, gate_matrix, (((1,), (1,)), ((), ())), preferr...  13.1 us
    dot_general x1, matrix products, expert_rows(): lax.dot_general(row_block, lift_matrix, (((1,), (1,)), ((), ())), preferr...  12.7 us
    all_to_all x2, blocking collectives, copy_for_each(): lax.all_to_all(jnp.broadcast_to(value[None], (size, *value.shape)), axis,...  12.6 us
    dot_general x1, matrix products, expert_rows(): return jnp.dot(hidden, down_matrix, preferred_element_type=jnp.float32)  11.5 us
  transfers between devices with their start and end apart: 3, of which 3 were waited for; matrix products, arithmetic and copies ran while one was open for 3% of the time, Pallas kernels for 0%

commit v1 on v0

v1 whole, which is shorter than its diff:
```python
import jax
import jax.numpy as jnp
from jax import lax
from jax.sharding import PartitionSpec as P

STEPS = 128
DISCOUNT = 0.99
EPSILON = 1e-05
HIGHEST = lax.Precision.HIGHEST


def retrace(action_values, actions, rewards, trace_codes):
    greedy = jnp.max(action_values, axis=1)
    picked = (
        actions[:, None] == jnp.arange(action_values.shape[1], dtype=jnp.int32)[None, :]
    ).astype(jnp.float32)
    taken = jnp.sum(action_values * picked, axis=1)
    trace = trace_codes.astype(jnp.float32) / 1024.0
    reward = rewards.astype(jnp.float32) * 0.25
    greedy = greedy.reshape(-1, STEPS)
    taken = taken.reshape(-1, STEPS)
    trace = trace.reshape(-1, STEPS)
    reward = reward.reshape(-1, STEPS)
    padding = jnp.zeros_like(greedy[:, :1])
    greedy_next = jnp.concatenate([greedy[:, 1:], padding], axis=1)
    taken_next = jnp.concatenate([taken[:, 1:], padding], axis=1)
    trace_next = jnp.concatenate([trace[:, 1:], padding], axis=1)
    driver = reward + DISCOUNT * (greedy_next - trace_next * taken_next)
    log_sums = jnp.cumsum(jnp.log(DISCOUNT * trace), axis=1)
    spans = log_sums[:, None, :] - log_sums[:, :, None]
    upper_mask = (
        jnp.arange(STEPS, dtype=jnp.int32)[None, :] >= jnp.arange(STEPS, dtype=jnp.int32)[:, None]
    )
    weight = jnp.where(upper_mask[None, :, :], jnp.exp(jnp.minimum(spans, 0.0)), 0.0)
    target = jnp.einsum("nts,ns->nt", weight, driver, precision=HIGHEST)
    return target.reshape(-1)


def rows_by(a, b):
    return lax.dot_general(a, b, (((1,), (1,)), ((), ())), preferred_element_type=jnp.float32)


def per_device(
    tokens,
    norm_gain,
    expert_ids,
    gate_codes,
    gate_weights,
    up_weights,
    down_weights,
    value_head,
    actions,
    rewards,
    trace_codes,
):
    dp, ex = lax.axis_size("dp"), lax.axis_size("expert")
    tp = lax.axis_size("tensor")
    rows, half = tokens.shape
    folded = jnp.dot(down_weights[0], value_head, preferred_element_type=jnp.float32)
    folded = folded.astype(jnp.bfloat16)
    wide = tokens.astype(jnp.float32)
    square = lax.psum(jnp.sum(wide * wide, axis=1, keepdims=True), "tensor") / (half * tp)
    gain = lax.dynamic_slice_in_dim(norm_gain, lax.axis_index("tensor") * half, half)
    normed = wide * lax.rsqrt(square + EPSILON) * gain.astype(jnp.float32)[None, :]
    normed = normed.astype(jnp.bfloat16)
    everyone = lax.all_gather(normed, ("dp", "expert", "tensor"), axis=0)
    everyone = everyone.reshape(dp * ex, tp, rows, half)
    left = everyone[:, 0].reshape(dp * ex * rows, half)
    right = everyone[:, 1].reshape(dp * ex * rows, half)
    gate_m, up_m = gate_weights[0], up_weights[0]
    gate = rows_by(left, gate_m[:, :half]) + rows_by(right, gate_m[:, half:])
    lift = rows_by(left, up_m[:, :half]) + rows_by(right, up_m[:, half:])
    hidden = (jax.nn.silu(gate) * lift).astype(jnp.bfloat16)
    value = jnp.dot(hidden, folded, preferred_element_type=jnp.float32)
    value = lax.psum_scatter(value, "dp", scatter_dimension=0, tiled=True)
    value = value.reshape(ex, rows, value.shape[1])
    value = lax.all_to_all(value, "expert", split_axis=0, concat_axis=0, tiled=True)
    codes = gate_codes.astype(jnp.float32)
    share = codes / jnp.sum(codes, axis=1, keepdims=True)
    named = expert_ids[None] == jnp.arange(ex, dtype=jnp.int32)[:, None, None]
    by_expert = jnp.sum(jnp.where(named, share[None], 0.0), axis=2)
    blended = jnp.sum(value * by_expert[:, :, None], axis=0)
    action_values = lax.psum(blended, "tensor")
    return action_values, retrace(action_values, actions, rewards, trace_codes)


def solution(mesh):
    group, weight = P(("dp", "expert"), None), P("expert", ("dp", "tensor"), None)
    line = P(("dp", "expert"))
    in_specs = (
        P(("dp", "expert"), "tensor"),
        P(),
        group,
        group,
        weight,
        weight,
        weight,
        P(),
        line,
        line,
        line,
    )
    return jax.shard_map(
        per_device, mesh=mesh, in_specs=in_specs, out_specs=(group, line), check_vma=False
    )
```

time: 328 us -> 305 us (0.930)
  waiting for transfers between devices: 237 us -> 213 us
  local copies, waits for them, and re-layouts: 4.22 us -> 20.6 us
  blocking collectives: 12.6 us -> 3.5 us
  starting transfers between devices: 10 us -> 4.22 us
    all_gather x1, waiting for transfers between devices: 219 us -> 108 us  [per_device(): everyone = lax.all_gather(normed, ('dp', 'expert', 'tensor'), axis=0)]
    reduce_scatter x0 -> x1, waiting for transfers between devices: none -> 75.6 us  [per_device(): value = lax.psum_scatter(value, 'dp', scatter_dimension=0, tiled=True)]
    psum x0 -> x1, waiting for transfers between devices: none -> 23.9 us  [per_device(): action_values = lax.psum(blended, 'tensor')]
    slice x2 -> x1, local copies, waits for them, and re-layouts: 0.18 us -> 18.8 us  [per_device(): right = everyone[:, 1].reshape(dp * ex * rows, half)]
    all_to_all x2 -> x1, waiting for transfers between devices: 18.5 us -> 5.52 us  [per_device(): lax.all_to_all(value, 'expert', split_axis=0, concat_axis=0, tiled=True)]
    all_to_all x2 -> x0, blocking collectives: 12.6 us -> none  [copy_for_each(): lax.all_to_all(jnp.broadcast_to(value[None], (size, *value.shape)), axis,...]
    all_to_all x2 -> x1, starting transfers between devices: 9.98 us -> 4.14 us  [per_device(): lax.all_to_all(value, 'expert', split_axis=0, concat_axis=0, tiled=True)]
    concatenate x1 -> x0, other arithmetic: 3.64 us -> none  [side_by_side(): both = jnp.concatenate(arrays, axis=along)]
  transfers between devices with their start and end apart: 3 -> 4, of which waited for: 3 -> 4; matrix products, arithmetic and copies ran while one was open for 3% -> 1% of each run, Pallas kernels for 0% -> 0%
where the time goes in v1:
time: 305 us; the launch traced here: 304 us
  waiting for transfers between devices  213 us (70%)
  matrix products  43.9 us (14%)
  local copies, waits for them, and re-layouts  20.6 us (7%)
  between operations  13.8 us (5%)
  other arithmetic  5.72 us (2%)
  starting transfers between devices  4.22 us (1%)
  blocking collectives  3.5 us (1%)
    all_gather x1, waiting for transfers between devices, per_device(): everyone = lax.all_gather(normed, ('dp', 'expert', 'tensor'), axis=0)  108 us
    reduce_scatter x1, waiting for transfers between devices, per_device(): value = lax.psum_scatter(value, 'dp', scatter_dimension=0, tiled=True)  75.6 us
    dot_general x3, matrix products, rows_by(): lax.dot_general(a, b, (((1,), (1,)), ((), ())), preferred_element_type=jn...  26.2 us
    psum x1, waiting for transfers between devices, per_device(): action_values = lax.psum(blended, 'tensor')  23.9 us
    slice x1, local copies, waits for them, and re-layouts, per_device(): right = everyone[:, 1].reshape(dp * ex * rows, half)  18.8 us
    dot_general x1, matrix products, per_device(): value = jnp.dot(hidden, folded, preferred_element_type=jnp.float32)  15.5 us
  transfers between devices with their start and end apart: 4, of which 4 were waited for; matrix products, arithmetic and copies ran while one was open for 1% of the time, Pallas kernels for 0%

profile of v1, /device:TPU:1, one launch (start us, length us, event | category | flops | bytes accessed | tf_op | source)
XLA Modules:
  0.0 304.3 jit_solution(3037245187421249182)
XLA Ops:
  7.2 0.0 copy-start
  7.2 0.0 all-gather.3.cloned.1.call-start
  7.2 1.2 fusion.4
  8.4 3.5 %psum.14 = f32[128,1]{0,1:T(1,128)S(1)} all-reduce(f32[128,1]{0,1:T(1,128)S(1)} %bitcast.47), channel_id=1, replica_groups=mesh['dp'=16,'expert'=4,'tensor'=2] {'tensor'}, use_global_device_ids=true, to_apply=%region_1.0 | all-reduce | flops 128 | bytes 1024 | tf_op jit(solution)/shard_map/psum | solution.py:62
  11.9 0.7 dynamic-slice_convert_fusion
  12.6 1.8 fusion.6
  14.4 0.0 all-gather.3.cloned.1.call-update
  14.4 0.0 reduce-scatter.2.cloned.1.call-start
  14.4 1.4 convolution_convert_fusion
  15.9 107.5 %all-gather.3.cloned.1.call-done = bf16[16384,1024]{1,0:T(8,128)(2,1)} async-done(((bf16[128,1024]{1,0:T(8,128)(2,1)}), bf16[16384,1024]{1,0:T(8,128)(2,1)}) %all-gather.3.cloned.1.call-update) | async-done | bytes 33554448 | tf_op jit(solution)/shard_map/all_gather | solution.py:66
  123.4 18.8 %fusion.36 = (bf16[64,1,128,1024]{3,2,1,0:T(8,128)(2,1)}, bf16[64,1,128,1024]{3,2,1,0:T(8,128)(2,1)S(1)}) fusion(bf16[64,2,128,1024]{3,2,1,0:T(8,128)(2,1)} %bitcast.39), kind=kLoop, calls=%fused_computation.58 | loop fusion | bytes 67108864 | tf_op jit(solution)/shard_map/slice | solution.py:69
  142.2 5.0 %fusion.12 = f32[8192,224]{0,1:T(8,128)S(1)} fusion(bf16[8192,1024]{1,0:T(8,128)(2,1)S(1)} %bitcast.35, bf16[224,2048]{1,0:T(8,128)(2,1)S(1)} %bitcast.40), kind=kOutput, calls=%fused_computation.17 | convolution fusion | flops 3758096384 | bytes 24576000 | tf_op jit(solution)/shard_map/dot_general | solution.py:40
  147.3 7.2 %fusion.9 = f32[8192,224]{0,1:T(8,128)} fusion(bf16[8192,1024]{1,0:T(8,128)(2,1)S(1)} %bitcast.36, bf16[224,2048]{1,0:T(8,128)(2,1)S(1)} %bitcast.43), kind=kOutput, calls=%fused_computation.14 | convolution fusion | flops 3758096384 | bytes 24576000 | tf_op jit(solution)/shard_map/dot_general | solution.py:40
  154.5 13.9 %convolution_add_fusion.1 = f32[8192,224]{0,1:T(8,128)} fusion(f32[8192,224]{0,1:T(8,128)S(1)} %fusion.12, bf16[8192,1024]{1,0:T(8,128)(2,1)} %bitcast.37, bf16[224,2048]{1,0:T(8,128)(2,1)S(1)} %bitcast.41), kind=kOutput, calls=%fused_computation.2 | convolution fusion | flops 3759931392 | bytes 31916032 | tf_op jit(solution)/shard_map/dot_general | solution.py:40
  168.4 0.0 copy-start.8
  168.4 0.0 copy-start.1
  168.5 15.5 %fusion.2 = f32[8192,128]{1,0:T(8,128)} fusion(bf16[224,128]{1,0:T(8,128)(2,1)S(1)} %convolution_convert_fusion, f32[8192,224]{0,1:T(8,128)} %fusion.9, bf16[8192,1024]{1,0:T(8,128)(2,1)} %bitcast.38, f32[8192,224]{0,1:T(8,128)} %convolution_add_fusion.1, bf16[224,2048]{1,0:T(8,128)(2,1)S(1)} %bitcast.44), kind=kOutput, calls=%fused_computation.4 | convolution fusion | flops 4240703488 | bytes 36167680 | tf_op jit(solution)/shard_map/dot_general | solution.py:74
  183.9 0.0 reduce-scatter.2.cloned.1.call-update
  184.0 75.6 %reduce-scatter.2.cloned.1.call-done = f32[512,128]{1,0:T(8,128)} async-done(((f32[8192,128]{1,0:T(8,128)}), f32[512,128]{1,0:T(8,128)}) %reduce-scatter.2.cloned.1.call-update) | async-done | bytes 262160 | tf_op jit(solution)/shard_map/reduce_scatter | solution.py:75
  259.6 4.1 %all-to-all-start = ((f32[4,128,128]{2,1,0:T(8,128)}), f32[4,128,128]{2,1,0:T(8,128)S(1)}, u32[]{:S(2)}, u32[]{:S(2)}) async-start(f32[4,128,128]{2,1,0:T(8,128)} %bitcast.42), calls=%async_computation.1 | async-start | bytes 524288 | tf_op jit(solution)/shard_map/all_to_all | solution.py:77
  263.7 5.5 %all-to-all-done = f32[4,128,128]{2,1,0:T(8,128)S(1)} async-done(((f32[4,128,128]{2,1,0:T(8,128)}), f32[4,128,128]{2,1,0:T(8,128)S(1)}, u32[]{:S(2)}, u32[]{:S(2)}) %all-to-all-start) | async-done | bytes 262176 | tf_op jit(solution)/shard_map/all_to_all | solution.py:77
  269.2 0.8 multiply_reduce_fusion
  270.0 0.0 all-reduce.2.cloned.1.call-update
  270.0 0.1 slice_bitcast_fusion.1
  270.1 0.1 copy.19
  270.2 0.2 reduce-window.7
  270.4 0.1 reduce
  270.5 23.9 %all-reduce.2.cloned.1.call-done = f32[128,128]{1,0:T(8,128)} async-done(((f32[128,128]{1,0:T(8,128)}), f32[128,128]{1,0:T(8,128)}) %all-reduce.2.cloned.1.call-update) | async-done | bytes 65552 | tf_op jit(solution)/shard_map/psum | solution.py:83
  294.4 1.0 select_reduce_fusion
  295.4 0.1 slice_bitcast_fusion
  295.5 0.8 convolution_bitcast_fusion
  296.3 1.5 copy.21
  (21 shorter events, 0.1 us)
Async XLA Ops:
  7.2 7.3 %copy-start = (bf16[1,224,2048]{2,1,0:T(8,128)(2,1)S(1)}, bf16[1,224,2048]{2,1,0:T(8,128)(2,1)}, u32[]{:S(2)}) copy-start(bf16[1,224,2048]{2,1,0:T(8,128)(2,1)} %param.17) | copy-start | bytes 2752516
  7.2 116.3 %all-gather.3.cloned.1.call-start = ((), (), s32[]{:S(2)}) async-start(), calls=%async_computation.4 | async-start | bytes 33816576 | tf_op jit(solution)/shard_map/all_gather | solution.py:66
  14.4 245.2 %reduce-scatter.2.cloned.1.call-start = ((), (), s32[]{:S(2)}) async-start(), calls=%async_computation.2 | async-start | bytes 4456448 | tf_op jit(solution)/shard_map/reduce_scatter | solution.py:75
  123.4 18.8 %copy-start.2 = (bf16[1,224,2048]{2,1,0:T(8,128)(2,1)S(1)}, bf16[1,224,2048]{2,1,0:T(8,128)(2,1)}, u32[]{:S(2)}) copy-start(bf16[1,224,2048]{2,1,0:T(8,128)(2,1)} %param.15) | copy-start | bytes 2752516
  142.2 5.1 %copy-start.3 = (bf16[1,224,2048]{2,1,0:T(8,128)(2,1)S(1)}, bf16[1,224,2048]{2,1,0:T(8,128)(2,1)}, u32[]{:S(2)}) copy-start(bf16[1,224,2048]{2,1,0:T(8,128)(2,1)} %param.16) | copy-start | bytes 2752516
  168.4 15.5 %copy-start.4 = (s32[128,2]{0,1:T(2,128)S(1)}, s32[128,2]{0,1:T(2,128)}, u32[]{:S(2)}) copy-start(s32[128,2]{0,1:T(2,128)} %param.14) | copy-start | bytes 3076
  168.4 15.6 %copy-start.5 = (s32[128,2]{0,1:T(2,128)S(1)}, s32[128,2]{0,1:T(2,128)}, u32[]{:S(2)}) copy-start(s32[128,2]{0,1:T(2,128)} %param.13) | copy-start | bytes 3076
  168.4 95.3 %copy-start.7 = (s32[128]{0:T(128)S(1)}, s32[128]{0:T(128)}, u32[]{:S(2)}) copy-start(s32[128]{0:T(128)} %param.21) | copy-start | bytes 1540
  168.4 126.0 %copy-start.6 = (s32[128]{0:T(128)S(1)}, s32[128]{0:T(128)}, u32[]{:S(2)}) copy-start(s32[128]{0:T(128)} %param.19) | copy-start | bytes 1540
  168.4 127.0 %copy-start.8 = (s32[128]{0:T(128)S(1)}, s32[128]{0:T(128)}, u32[]{:S(2)}) copy-start(s32[128]{0:T(128)} %param.20) | copy-start | bytes 1540
  168.4 129.3 %copy-start.1 = (bf16[1,224,2048]{2,1,0:T(8,128)(2,1)S(1)}, bf16[1,224,2048]{2,1,0:T(8,128)(2,1)}, u32[]{:S(2)}) copy-start(bf16[1,224,2048]{2,1,0:T(8,128)(2,1)} %param.17) | copy-start | bytes 2752516
  259.6 9.7 %all-to-all-start = ((f32[4,128,128]{2,1,0:T(8,128)}), f32[4,128,128]{2,1,0:T(8,128)S(1)}, u32[]{:S(2)}, u32[]{:S(2)}) async-start(f32[4,128,128]{2,1,0:T(8,128)} %bitcast.42), calls=%async_computation.1 | async-start | bytes 524288 | tf_op jit(solution)/shard_map/all_to_all | solution.py:77
  263.7 30.7 %all-reduce.2.cloned.1.call-start = ((), (), s32[]{:S(2)}) async-start(), calls=%async_computation.3 | async-start | bytes 131072 | tf_op jit(solution)/shard_map/psum | solution.py:83
Sparse Core Ops, SparseCore 0:
  14.5 108.8 all-gather.2
  184.1 75.4 reduce-scatter.1
  270.1 24.1 all-reduce.1

commit v2 on v1

v2 whole, which is shorter than its diff:
```python
import functools

import jax
import jax.numpy as jnp
from jax import lax
from jax.experimental import pallas as pl
from jax.experimental.pallas import tpu as pltpu
from jax.sharding import PartitionSpec as P

DISCOUNT = 0.99
EPSILON = 1e-05
MESH = pl.DeviceIdType.MESH
F32, BF16 = jnp.float32, jnp.bfloat16

OFFSET = (0, 3, 1, 2)
SEEN_AS = (0, 2, 1, 3)
ROW_A = 48
WEIGHT_ROWS = ((0, 32), (32, 64), (96, 64), (160, 64))


def rows_by(a, b):
    return lax.dot_general(a, b, (((1,), (1,)), ((), ())), preferred_element_type=F32)


def silu(v):
    return v / (1.0 + jnp.exp(-v))


def both(*key):
    return [(*key, 0), (*key, 1)]


def plan():
    first = [("w", 0)]
    first += [("r", 0, 1, 0, 0), ("r", 0, 2, 0, 1), ("r", 0, 0, 1, 0), ("r", 0, 0, 2, 1)]
    first += [("r", 0, 1, 0, 1), ("r", 0, 2, 0, 0), ("r", 0, 0, 1, 1), ("r", 0, 0, 2, 0)]
    first += [("r", 1, 0, 0, 0), ("r", 1, 0, 0, 1)]
    first += both("r", 0, 3, 0)
    first += [("r", 1, 1, 0, 0), ("r", 1, 2, 0, 1), ("r", 1, 1, 0, 1), ("r", 1, 2, 0, 0)]
    first += both("r", 0, 0, 3) + [("s", 0)]
    first += both("r", 1, 3, 0) + [("d",), ("p", 0)]

    def line(g, l):
        out = [("r", g, l, 1, 0), ("r", g, l, 2, 1), ("r", g, l, 1, 1), ("r", g, l, 2, 0)]
        return out + both("r", g, l, 3) + ([("s", l)] if g == 0 else [("b", l)])

    before_one = {0: first, 1: line(0, 1), 2: line(0, 2) + [("w", 1)], 3: line(0, 3)}
    before_one |= {4: line(1, 0), 5: line(1, 1) + [("w", 2)], 6: line(1, 2), 7: line(1, 3)}
    before_two = {0: [("p", 1)], 3: [("p", 2)], 8: [("w", 3), ("p", 3)]}
    return before_one, before_two


UNITS = ((0, 4), (1, 4), (2, 4), (0, 5), (1, 5), (2, 5), (3, 4), (3, 5), (0, 6), (1, 6), (2, 6), (3, 6))
UNITS_AFTER = {3: (0, 2), 5: (2, 5), 6: (5, 6), 7: (6, 12)}


def pick(index, values):
    out = values[-1]
    for i in range(len(values) - 2, -1, -1):
        out = jnp.where(index == i, values[i], out)
    return out


def kernel(
    tokens_ref,
    gain_ref,
    ids_ref,
    codes_ref,
    gate_ref,
    up_ref,
    down_ref,
    head_ref,
    actions_ref,
    rewards_ref,
    trace_ref,
    values_ref,
    targets_ref,
    tin,
    rin,
    tok,
    wb,
    down_v,
    head_v,
    folded,
    heads,
    acc,
    stage,
    parts,
    final,
    local_sem,
    raw_sem,
    tok_recv,
    tok_send,
    b_recv,
    b_send,
    w_recv,
    w_send,
    d_recv,
    d_send,
    rs_recv,
    rs_send,
    fin_sem,
):
    dp, z, c = lax.axis_index("dp"), lax.axis_index("expert"), lax.axis_index("tensor")
    x, y = dp % 4, dp // 4
    x_one = x + 1 - 2 * (x % 2)
    x_two = (x + 2 * (x % 2) + 3) % 4
    first, second = y * (1 - c) + z * c, z * (1 - c) + y * c

    def device(x_, f_, s_):
        y_, z_ = f_ * (1 - c) + s_ * c, s_ * (1 - c) + f_ * c
        return (y_ * 4 + x_, z_, c)

    partner = (dp, z, 1 - c)
    other = (y * 4 + x_one, z, c)
    twin = device(x_two, first, second)
    f_next = device(x, (first + 1) % 4, second)
    f_prev = device(x, (first + 3) % 4, second)
    s_next = device(x, first, (second + 1) % 4)
    s_prev = device(x, first, (second + 3) % 4)

    def remote(src, dst, send, recv, to):
        return pltpu.make_async_remote_copy(
            src_ref=src, dst_ref=dst, send_sem=send, recv_sem=recv, device_id=to, device_id_type=MESH
        )

    loads = [pltpu.make_async_copy(tokens_ref.at[pl.ds(i * 64, 64)], tin.at[i], local_sem.at[i]) for i in range(2)]
    w_loads = []
    for n, (at, size) in enumerate(WEIGHT_ROWS):
        chunk = n - 1 if n else 3
        for i, ref in enumerate((gate_ref, up_ref)):
            w_loads.append(
                pltpu.make_async_copy(
                    ref.at[0, pl.ds(at, size)], wb.at[chunk, pl.ds(i * 128, size)], local_sem.at[2 + 2 * n + i]
                )
            )
    d_loads = [
        pltpu.make_async_copy(down_ref.at[0], down_v, local_sem.at[10]),
        pltpu.make_async_copy(head_ref, head_v, local_sem.at[11]),
    ]
    for copy in loads + w_loads + d_loads:
        copy.start()

    barrier = pltpu.get_barrier_semaphore()
    count = 2
    for to in (partner, other):
        pl.semaphore_signal(barrier, inc=1, device_id=to, device_id_type=MESH)
    for g in range(2):
        for l in range(4):
            for s in range(4):
                if (g, l, s) == (0, 0, 0):
                    continue
                to = device(x_two if g else x, (first + OFFSET[l]) % 4, (second + OFFSET[s]) % 4)
                pl.semaphore_signal(barrier, inc=1, device_id=to, device_id_type=MESH)
                count += 1
    for copy in loads:
        copy.wait()
    pl.semaphore_wait(barrier, count)

    sends = []

    def start(make, *args):
        make(*args).start()
        sends.append((make, args))

    def raw_copy():
        return remote(tin.at[1 - c], rin, raw_sem.at[0], raw_sem.at[1], partner)

    start(raw_copy)
    for copy in w_loads:
        copy.wait()

    def weight_copy(n, i, role):
        size = WEIGHT_ROWS[n][1]
        mine, theirs = (n - 1, n + 3) if n else (3, 3)
        if role == 0:
            src, dst, at, to = mine, mine, (0, size), partner
        elif role == 1:
            src, dst, at, to = mine, theirs, (0, 0 if n else 2 * size), other
        else:
            src, dst, at, to = theirs, theirs, (0, size) if n else (2 * size, 3 * size), partner
        return remote(
            wb.at[src, pl.ds(i * 128 + at[0], size)],
            wb.at[dst, pl.ds(i * 128 + at[1], size)],
            w_send.at[role, n, i],
            w_recv.at[role, n, i],
            to,
        )

    for i in range(2):
        start(weight_copy, 0, i, 1)
    for n in range(4):
        for i in range(2):
            start(weight_copy, n, i, 0)

    raw_copy().wait_recv()
    mine = tin[c].astype(F32)
    theirs = rin[...].astype(F32)
    square = jnp.sum(mine * mine, axis=1, keepdims=True) + jnp.sum(theirs * theirs, axis=1, keepdims=True)
    scaling = lax.rsqrt(square / 2048.0 + EPSILON)
    for part, at in ((mine, c), (theirs, 1 - c)):
        lanes = pl.ds(pl.multiple_of(at * 1024, 1024), 1024)
        gain = gain_ref[:, lanes].astype(F32)
        tok[0, pl.ds(0, 64), lanes] = (part * scaling * gain).astype(BF16)

    def block(g, l, s, h):
        return tok.at[4 * g + l, pl.ds(64 * s, 64 if g == 0 else ROW_A), pl.ds(1024 * h, 1024)]

    def token_copy(g, src, dst, h, to):
        return remote(
            block(g, *src, h), block(g, *dst, h), tok_send.at[g, *dst, h], tok_recv.at[g, *dst, h], to
        )

    def along_second(g, l, h):
        start(token_copy, g, (l, 0), (l, 1), h, s_next)
        start(token_copy, g, (l, 0), (l, 2), h, s_prev)

    def along_first(g, h, up):
        if up:
            start(token_copy, g, (0, 0), (1, 0), h, f_next)
        else:
            start(token_copy, g, (0, 0), (2, 0), h, f_prev)

    def edge(ref, l, s):
        return ref.at[l, pl.ds(64 * s + ROW_A, 64 - ROW_A)]

    def edge_copy(l, s):
        return remote(edge(tok, l, s), edge(tok, 4 + l, s), b_send.at[l, s], b_recv.at[l, s], twin)

    def twin_copy(h):
        src = tok.at[0, pl.ds(0, ROW_A), pl.ds(1024 * h, 1024)]
        return remote(src, block(1, 0, 0, h), tok_send.at[1, 0, 0, h], tok_recv.at[1, 0, 0, h], twin)

    for h in range(2):
        along_first(0, h, True)
        along_first(0, 1 - h, False)
        start(twin_copy, h)
        start(token_copy, 0, (0, 0), (0, 1), h, s_next)
        start(token_copy, 0, (0, 0), (0, 2), 1 - h, s_prev)
    start(edge_copy, 0, 0)

    for copy in d_loads:
        copy.wait()
    folded[0] = jnp.dot(down_v[...], head_v[...], preferred_element_type=F32).astype(BF16)

    def head_copy(role):
        src, dst, to = ((0, 1, partner), (0, 2, other), (2, 3, partner))[role]
        return remote(folded.at[src], folded.at[dst], d_send.at[role], d_recv.at[role], to)

    start(head_copy, 1)
    start(head_copy, 0)
    for n in range(1, 4):
        for i in range(2):
            start(weight_copy, n, i, 1)

    def happen(event):
        kind = event[0]
        if kind == "r":
            _, g, l, s, h = event
            copy = token_copy(g, (l, s), (l, s), h, partner)
            copy.wait_recv()
            if s == 0:
                if l == 0:
                    along_first(g, h, True)
                    along_first(g, h, False)
                if (l, h) == (1, 0):
                    start(token_copy, g, (1, 0), (3, 0), 0, f_next)
                if (l, h) == (2, 1):
                    start(token_copy, g, (2, 0), (3, 0), 1, f_prev)
                along_second(g, l, h)
            if (s, h) == (1, 0):
                start(token_copy, g, (l, 1), (l, 3), 0, s_next)
            if (s, h) == (2, 1):
                start(token_copy, g, (l, 2), (l, 3), 1, s_prev)
        elif kind == "s":
            for s in range(4):
                if (event[1], s) != (0, 0):
                    start(edge_copy, event[1], s)
        elif kind == "b":
            for s in range(4):
                edge_copy(event[1], s).wait_recv()
        elif kind == "w":
            for i in range(2):
                weight_copy(event[1], i, 1).wait_recv()
                start(weight_copy, event[1], i, 2)
        elif kind == "p":
            for i in range(2):
                weight_copy(event[1], i, 2).wait_recv()
        else:
            head_copy(1).wait_recv()
            start(head_copy, 2)
            head_copy(0).wait_recv()
            head_copy(2).wait_recv()
            for n in range(4):
                at, size = WEIGHT_ROWS[n]
                if n == 0:
                    for j in range(4):
                        heads[3, pl.ds(32 * j, 32)] = folded[j, pl.ds(at, size)]
                else:
                    for j in range(4):
                        heads[n - 1 + 4 * (j // 2), pl.ds(64 * (j % 2), 64)] = folded[j, pl.ds(at, size)]

    before_one, before_two = plan()
    for n in range(4):
        for i in range(2):
            weight_copy(n, i, 0).wait_recv()
    for event in before_one[0]:
        happen(event)

    def unit_one(b):
        product = rows_by(tok[b], wb[0:4].reshape(1024, 2048))
        hidden = [
            (silu(product[:, 256 * k : 256 * k + 128]) * product[:, 256 * k + 128 : 256 * k + 256]).astype(BF16)
            for k in range(4)
        ]
        acc[pl.ds(pl.multiple_of(256 * b, 256), 256)] = jnp.dot(
            jnp.concatenate(hidden, axis=1), heads[0:4].reshape(512, 128), preferred_element_type=F32
        )

    def unit_two(p, k):
        product = rows_by(tok[pl.ds(2 * p, 2)].reshape(512, 2048), wb[k])
        hidden = (silu(product[:, :128]) * product[:, 128:]).astype(BF16)
        rows = pl.ds(pl.multiple_of(512 * p, 512), 512)
        total = acc[rows] + jnp.dot(hidden, heads[k], preferred_element_type=F32)
        acc[rows] = total
        return total

    def part_copy(p, r, s):
        g, q = p // 2, p % 2
        to = device(
            x + g * (x_two - x), (first + q + r * (3 - 2 * q)) % 4, (second + OFFSET[s]) % 4
        )
        src = stage.at[2 * p + r, pl.ds(64 * s, 64)]
        slot = g * 16 + (q + 2 * r) * 4 + SEEN_AS[s]
        return remote(src, parts.at[slot], rs_send.at[slot], rs_recv.at[slot], to)

    def step(j, _):
        for i in range(1, 8):

            @pl.when(j == i)
            def _():
                for event in before_one[i]:
                    happen(event)

        unit_one(j)

        def inner(u, _):
            for i, events in before_two.items():

                @pl.when(u == i)
                def _():
                    for event in events:
                        happen(event)

            p, k = pick(u, [v[0] for v in UNITS]), pick(u, [v[1] for v in UNITS])
            total = unit_two(p, k)

            @pl.when(u >= 8)
            def _():
                stage[pl.ds(2 * p, 2)] = total.astype(BF16).reshape(2, 256, 128)
                for r in range(2):
                    for s in range(4):
                        if (r, s) == (0, 0):

                            @pl.when(p > 0)
                            def _():
                                part_copy(p, 0, 0).start()

                        else:
                            part_copy(p, r, s).start()

            return 0

        low = pick(j, [UNITS_AFTER.get(i, (0, 0))[0] for i in range(8)])
        high = pick(j, [UNITS_AFTER.get(i, (0, 0))[1] for i in range(8)])
        lax.fori_loop(low, high, inner, 0)
        return 0

    lax.fori_loop(0, 8, step, 0)

    codes = codes_ref[pl.ds(pl.multiple_of(64 * c, 64), 64), :].astype(F32)
    ids = ids_ref[pl.ds(pl.multiple_of(64 * c, 64), 64), :]
    share = codes / (codes[:, 0:1] + codes[:, 1:2])
    shares = []
    for j in range(4):
        named = ids == (z + OFFSET[j]) % 4
        picked = jnp.where(named, share, 0.0)
        shares.append(picked[:, 0:1] + picked[:, 1:2])
    c_wide = c.astype(F32)

    for slot in range(1, 32):
        remote(parts.at[slot], parts.at[slot], rs_send.at[slot], rs_recv.at[slot], partner).wait_recv()
    blended = jnp.zeros((64, 128), F32)
    for l in range(4):
        for s in range(4):
            slot = 4 * l + s
            near = parts[slot].astype(F32) if slot else acc[0:64]
            weight = shares[s] * (1.0 - c_wide) + shares[l] * c_wide
            blended += (near + parts[16 + slot].astype(F32)) * weight
    final[c] = blended

    def final_copy():
        return remote(final.at[c], final.at[c], fin_sem.at[0], fin_sem.at[1], partner)

    start(final_copy)
    final_copy().wait_recv()
    values = final[...].reshape(128, 128)
    values_ref[...] = values

    lane = lax.broadcasted_iota(jnp.int32, (128, 128), 1)
    row = lax.broadcasted_iota(jnp.int32, (128, 128), 0)

    def column(v):
        return jnp.sum(jnp.where(lane == row, v, 0.0), axis=1, keepdims=True)

    trace = trace_ref[...].astype(F32) / 1024.0
    reward = rewards_ref[...].astype(F32) * 0.25
    action_column = jnp.sum(jnp.where(lane == row, actions_ref[...], 0), axis=1, keepdims=True)
    greedy = jnp.max(values, axis=1, keepdims=True)
    taken = jnp.sum(jnp.where(lane == action_column, values, 0.0), axis=1, keepdims=True)
    ahead = greedy - column(trace) * taken
    driver = reward + DISCOUNT * jnp.sum(jnp.where(row == lane + 1, ahead, 0.0), axis=0, keepdims=True)
    logs = jnp.log(DISCOUNT * trace)
    sums_column = jnp.sum(jnp.where(lane <= row, logs, 0.0), axis=1, keepdims=True)
    sums_row = jnp.sum(jnp.where(lane == row, sums_column, 0.0), axis=0, keepdims=True)
    weight = jnp.where(lane >= row, jnp.exp(jnp.minimum(sums_row - sums_column, 0.0)), 0.0)
    target = jnp.sum(weight * driver, axis=1, keepdims=True)
    targets_ref[...] = jnp.sum(jnp.where(lane == row, target, 0.0), axis=0, keepdims=True)

    for make, args in sends:
        make(*args).wait_send()
    for slot in range(1, 32):
        remote(parts.at[slot], parts.at[slot], rs_send.at[slot], rs_recv.at[slot], partner).wait_send()


def per_device(
    tokens,
    norm_gain,
    expert_ids,
    gate_codes,
    gate_weights,
    up_weights,
    down_weights,
    value_head,
    actions,
    rewards,
    trace_codes,
):
    dma = pltpu.SemaphoreType.DMA
    vmem, hbm = pl.BlockSpec(memory_space=pltpu.VMEM), pl.BlockSpec(memory_space=pl.ANY)
    values, targets = pl.pallas_call(
        kernel,
        out_shape=(jax.ShapeDtypeStruct((128, 128), F32), jax.ShapeDtypeStruct((1, 128), F32)),
        in_specs=[hbm, vmem, vmem, vmem, hbm, hbm, hbm, hbm, vmem, vmem, vmem],
        out_specs=(vmem, vmem),
        scratch_shapes=[
            pltpu.VMEM((2, 64, 1024), BF16),
            pltpu.VMEM((64, 1024), BF16),
            pltpu.VMEM((8, 256, 2048), BF16),
            pltpu.VMEM((7, 256, 2048), BF16),
            pltpu.VMEM((224, 2048), BF16),
            pltpu.VMEM((2048, 128), BF16),
            pltpu.VMEM((4, 224, 128), BF16),
            pltpu.VMEM((7, 128, 128), BF16),
            pltpu.VMEM((2048, 128), F32),
            pltpu.VMEM((8, 256, 128), BF16),
            pltpu.VMEM((32, 64, 128), BF16),
            pltpu.VMEM((2, 64, 128), F32),
            dma((12,)),
            dma((2,)),
            dma((2, 4, 4, 2)),
            dma((2, 4, 4, 2)),
            dma((4, 4)),
            dma((4, 4)),
            dma((3, 4, 2)),
            dma((3, 4, 2)),
            dma((3,)),
            dma((3,)),
            dma((32,)),
            dma((32,)),
            dma((2,)),
        ],
        compiler_params=pltpu.CompilerParams(
            collective_id=0, has_side_effects=True, vmem_limit_bytes=56 * 1024 * 1024
        ),
        name="critic",
    )(
        tokens,
        norm_gain.reshape(1, -1),
        expert_ids,
        gate_codes,
        gate_weights,
        up_weights,
        down_weights,
        value_head,
        actions.reshape(1, -1),
        rewards.reshape(1, -1),
        trace_codes.reshape(1, -1),
    )
    return values, targets.reshape(-1)


def solution(mesh):
    group, weight = P(("dp", "expert"), None), P("expert", ("dp", "tensor"), None)
    line = P(("dp", "expert"))
    in_specs = (
        P(("dp", "expert"), "tensor"),
        P(),
        group,
        group,
        weight,
        weight,
        weight,
        P(),
        line,
        line,
        line,
    )
    return jax.shard_map(
        per_device, mesh=mesh, in_specs=in_specs, out_specs=(group, line), check_vma=False
    )
```

time: 305 us -> 112 us (0.37)
  waiting for transfers between devices: 213 us -> 0 us
  Pallas kernels: 0 us -> 106 us
  matrix products: 43.9 us -> 0 us
  local copies, waits for them, and re-layouts: 20.6 us -> 4.83 us
  between operations: 13.8 us -> 0.66 us
  other arithmetic: 5.72 us -> 0 us
  starting transfers between devices: 4.22 us -> 0 us
  blocking collectives: 3.5 us -> 0 us
    all_gather x1 -> x0, waiting for transfers between devices: 108 us -> none  [per_device(): everyone = lax.all_gather(normed, ('dp', 'expert', 'tensor'), axis=0)]
    pallas_call x0 -> x1, Pallas kernels: none -> 106 us  [per_device(): pl.pallas_call(kernel, out_shape=(jax.ShapeDtypeStruct((128, 128), F32),...]
    reduce_scatter x1 -> x0, waiting for transfers between devices: 75.6 us -> none  [per_device(): value = lax.psum_scatter(value, 'dp', scatter_dimension=0, tiled=True)]
    dot_general x6 -> x0, matrix products: 43.9 us -> none  [the longest x3 26.2 us: rows_by(): lax.dot_general(a, b, (((1,), (1,)), ((), ())), preferred_element_type=jn...]
    psum x1 -> x0, waiting for transfers between devices: 23.9 us -> none  [per_device(): action_values = lax.psum(blended, 'tensor')]
    slice x1 -> x0, local copies, waits for them, and re-layouts: 18.8 us -> none  [per_device(): right = everyone[:, 1].reshape(dp * ex * rows, half)]
    all_to_all x1 -> x0, waiting for transfers between devices: 5.52 us -> none  [per_device(): lax.all_to_all(value, 'expert', split_axis=0, concat_axis=0, tiled=True)]
    all_to_all x1 -> x0, starting transfers between devices: 4.14 us -> none  [per_device(): lax.all_to_all(value, 'expert', split_axis=0, concat_axis=0, tiled=True)]
  transfers between devices with their start and end apart: 4 -> 0, of which waited for: 4 -> 0; matrix products, arithmetic and copies ran while one was open for 1% -> 0% of each run, Pallas kernels for 0% -> 0%
where the time goes in v2:
time: 112 us
  Pallas kernels  106 us (95%)
  local copies, waits for them, and re-layouts  4.83 us (4%)
    pallas_call x1, Pallas kernels, per_device(): pl.pallas_call(kernel, out_shape=(jax.ShapeDtypeStruct((128, 128), F32),...  106 us
    unnamed x12, local copies, waits for them, and re-layouts  4.23 us

profile of v2, /device:TPU:1, one launch (start us, length us, event | category | flops | bytes accessed | tf_op | source)
XLA Modules:
  0.0 111.8 jit_solution(13203281096706396945)
XLA Ops:
  0.6 0.0 copy-start
  0.6 0.7 copy-done
  1.3 0.0 copy-start.1
  1.3 0.6 reshape.19.gain_ref
  1.9 0.1 copy-done.1
  2.0 0.0 copy-start.2
  2.0 0.7 copy.13.ids_ref
  2.7 0.0 copy-done.2
  2.7 0.7 copy.14.codes_ref
  3.5 106.3 %critic.1 = (f32[128,128]{1,0:T(8,128)}, f32[1,128]{1,0:T(1,128)}) custom-call(bf16[128,1024]{1,0:T(8,128)(2,1)} %tokens_ref.1, bf16[1,2048]{1,0:T(2,128)(2,1)} %reshape.19.gain_ref, s32[128,2]{1,0:T(8,128)} %copy.13.ids_ref, s32[128,2]{1,0:T(8,128)} %copy.14.codes_ref, bf16[1,224,2048]{2,1,0:T(8,128)(2,1)} %gate_ref.1, bf16[1,224,2048]{2,1,0:T(8,128)(2,1)} %up_ref.1, ...), custom_call_target="tpu_custom_call" | custom-call | tf_op jit(solution)/shard_map/critic/pallas_call | solution.py:451
  109.8 0.0 copy-start.3
  109.8 1.5 %copy.17 = f32[128,128]{1,0:T(8,128)} copy(f32[128,128]{1,0:T(8,128)} %get-tuple-element.8) | data formatting | bytes 131072
  111.3 0.0 copy-done.3
  111.3 0.5 copy.18
Async XLA Ops:
  0.6 0.7 copy-start
  1.3 0.7 copy-start.1
  2.0 0.7 copy-start.2
  109.8 1.5 %copy-start.3 = (f32[1,128]{1,0:T(1,128)S(1)}, f32[1,128]{1,0:T(1,128)}, u32[]{:S(2)}) copy-start(f32[1,128]{1,0:T(1,128)} %get-tuple-element.5) | copy-start | bytes 1540

commit v3 on v2

--- a/solution.py
+++ b/solution.py
@@ -26,32 +26,138 @@
     return v / (1.0 + jnp.exp(-v))
 
 
-def both(*key):
-    return [(*key, 0), (*key, 1)]
-
-
-def plan():
-    first = [("w", 0)]
-    first += [("r", 0, 1, 0, 0), ("r", 0, 2, 0, 1), ("r", 0, 0, 1, 0), ("r", 0, 0, 2, 1)]
-    first += [("r", 0, 1, 0, 1), ("r", 0, 2, 0, 0), ("r", 0, 0, 1, 1), ("r", 0, 0, 2, 0)]
-    first += [("r", 1, 0, 0, 0), ("r", 1, 0, 0, 1)]
-    first += both("r", 0, 3, 0)
-    first += [("r", 1, 1, 0, 0), ("r", 1, 2, 0, 1), ("r", 1, 1, 0, 1), ("r", 1, 2, 0, 0)]
-    first += both("r", 0, 0, 3) + [("s", 0)]
-    first += both("r", 1, 3, 0) + [("d",), ("p", 0)]
-
-    def line(g, l):
-        out = [("r", g, l, 1, 0), ("r", g, l, 2, 1), ("r", g, l, 1, 1), ("r", g, l, 2, 0)]
-        return out + both("r", g, l, 3) + ([("s", l)] if g == 0 else [("b", l)])
-
-    before_one = {0: first, 1: line(0, 1), 2: line(0, 2) + [("w", 1)], 3: line(0, 3)}
-    before_one |= {4: line(1, 0), 5: line(1, 1) + [("w", 2)], 6: line(1, 2), 7: line(1, 3)}
-    before_two = {0: [("p", 1)], 3: [("p", 2)], 8: [("w", 3), ("p", 3)]}
-    return before_one, before_two
-
-
-UNITS = ((0, 4), (1, 4), (2, 4), (0, 5), (1, 5), (2, 5), (3, 4), (3, 5), (0, 6), (1, 6), (2, 6), (3, 6))
-UNITS_AFTER = {3: (0, 2), 5: (2, 5), 6: (5, 6), 7: (6, 12)}
+ORDER = (
+    (
+        (
+            ("r", 1, 0, 0, 0), ("q", 1, 0, 0), ("r", 0, 1, 0, 0), ("q", 0, 1, 0), ("r", 0, 2, 0, 1),
+            ("r", 0, 0, 1, 0), ("r", 0, 0, 2, 1), ("r", 1, 0, 0, 1), ("f", 0, 0, 0), ("f", 0, 0, 1),
+            ("r", 0, 1, 0, 1), ("e", 1, 0), ("r", 0, 2, 0, 0), ("e", 2, 0), ("r", 0, 0, 1, 1), ("e", 0, 1),
+            ("r", 0, 0, 2, 0), ("e", 0, 2), ("w", 0), ("B", 0, 0), ("w", "d"), ("q", 0, 1, 1), ("p", 0),
+            ("r", 1, 1, 0, 0), ("r", 1, 2, 0, 0), ("r", 1, 0, 1, 0), ("r", 1, 0, 2, 0), ("p", "d"),
+            ("B", 1, 0), ("q", 0, 2, 1), ("B", 2, 0), ("r", 0, 3, 0, 0), ("r", 0, 3, 0, 1), ("e", 3, 0),
+            ("r", 0, 1, 1, 0), ("r", 0, 1, 2, 0), ("B", 0, 1), ("r", 1, 1, 0, 1), ("r", 1, 2, 0, 1),
+            ("q", 0, 2, 0), ("r", 0, 0, 3, 1), ("B", 0, 2), ("r", 0, 0, 3, 0), ("e", 0, 3),
+        ),
+        (0,),
+    ),
+    (
+        (
+            ("f", 0, 1, 0), ("r", 0, 1, 2, 1), ("e", 1, 2), ("f", 0, 1, 1), ("B", 3, 0), ("r", 1, 3, 0, 0),
+            ("r", 0, 1, 1, 1), ("e", 1, 1), ("q", 0, 3, 0), ("B", 0, 3), ("r", 1, 3, 0, 1), ("r", 0, 2, 1, 1),
+            ("r", 0, 2, 2, 1), ("q", 0, 3, 1), ("w", 1), ("B", 1, 2), ("r", 0, 2, 1, 0), ("e", 2, 1),
+            ("r", 0, 2, 2, 0), ("e", 2, 2), ("f", 0, 2, 1), ("f", 0, 2, 0), ("B", 1, 1), ("r", 0, 1, 3, 0),
+            ("r", 0, 1, 3, 1), ("e", 1, 3),
+        ),
+        (1,),
+    ),
+    (
+        (
+            ("q", 1, 0, 1), ("q", 1, 1, 0), ("p", 1), ("r", 0, 3, 1, 0), ("r", 0, 3, 2, 0),
+        ),
+        (0, 4),
+    ),
+    (
+        (
+            ("f", 0, 3, 0), ("B", 2, 1), ("r", 0, 3, 1, 1), ("e", 3, 1), ("r", 0, 3, 2, 1), ("e", 3, 2),
+            ("f", 0, 3, 1), ("B", 2, 2), ("q", 1, 1, 1), ("r", 0, 2, 3, 0), ("r", 0, 2, 3, 1), ("e", 2, 3),
+        ),
+        (2,),
+    ),
+    (
+        (
+            ("f", 1, 0, 0), ("q", 1, 2, 0), ("B", 1, 3), ("r", 1, 0, 1, 1), ("r", 1, 0, 2, 1), ("f", 1, 0, 1),
+            ("B", 3, 1), ("r", 1, 1, 1, 0), ("r", 1, 1, 2, 0), ("q", 1, 2, 1), ("B", 3, 2), ("r", 0, 3, 3, 0),
+            ("r", 0, 3, 3, 1), ("e", 3, 3),
+        ),
+        (3,),
+    ),
+    (
+        (
+            ("f", 1, 1, 0), ("q", 1, 3, 0), ("r", 1, 1, 1, 1), ("r", 1, 1, 2, 1), ("f", 1, 1, 1), ("B", 2, 3),
+        ),
+        (1, 4),
+    ),
+    (
+        (
+            ("q", 1, 3, 1), ("w", 2), ("r", 1, 0, 3, 0), ("r", 1, 2, 2, 0), ("r", 1, 2, 1, 0),
+            ("r", 1, 0, 3, 1),
+        ),
+        (4,),
+    ),
+    (
+        (
+            ("f", 1, 2, 0), ("B", 3, 3), ("r", 1, 2, 1, 1), ("r", 1, 2, 2, 1), ("f", 1, 2, 1), ("p", 2),
+        ),
+        (0, 5),
+    ),
+    (
+        (
+            ("r", 1, 1, 3, 0), ("r", 1, 3, 2, 0),
+        ),
+        (1, 5),
+    ),
+    (
+        (
+            ("r", 1, 3, 1, 0), ("f", 1, 3, 0), ("r", 1, 1, 3, 1),
+        ),
+        (5,),
+    ),
+    (
+        (
+            ("r", 1, 3, 1, 1), ("r", 1, 3, 2, 1), ("f", 1, 3, 1), ("r", 1, 2, 3, 0), ("r", 1, 2, 3, 1),
+        ),
+        (6,),
+    ),
+    (
+        (
+            ("r", 1, 3, 3, 0),
+        ),
+        (2, 4),
+    ),
+    (
+        (
+        ),
+        (2, 5),
+    ),
+    (
+        (
+            ("r", 1, 3, 3, 1),
+        ),
+        (7,),
+    ),
+    (
+        (
+            ("w", 3),
+        ),
+        (3, 4),
+    ),
+    (
+        (
+        ),
+        (3, 5),
+    ),
+    (
+        (
+            ("p", 3),
+        ),
+        (0, 6),
+    ),
+    (
+        (
+        ),
+        (1, 6),
+    ),
+    (
+        (
+        ),
+        (2, 6),
+    ),
+    (
+        (
+        ),
+        (3, 6),
+    ),
+)
 
 
 def pick(index, values):
@@ -70,11 +176,7 @@
     up_ref,
     down_ref,
     head_ref,
-    actions_ref,
-    rewards_ref,
-    trace_ref,
-    values_ref,
-    targets_ref,
+    final_ref,
     tin,
     rin,
     tok,
@@ -86,7 +188,7 @@
     acc,
     stage,
     parts,
-    final,
+    gain_v,
     local_sem,
     raw_sem,
     tok_recv,
@@ -142,20 +244,11 @@
         copy.start()
 
     barrier = pltpu.get_barrier_semaphore()
-    count = 2
-    for to in (partner, other):
+    for to in (partner, other, twin, f_next, f_prev, s_next, s_prev):
         pl.semaphore_signal(barrier, inc=1, device_id=to, device_id_type=MESH)
-    for g in range(2):
-        for l in range(4):
-            for s in range(4):
-                if (g, l, s) == (0, 0, 0):
-                    continue
-                to = device(x_two if g else x, (first + OFFSET[l]) % 4, (second + OFFSET[s]) % 4)
-                pl.semaphore_signal(barrier, inc=1, device_id=to, device_id_type=MESH)
-                count += 1
     for copy in loads:
         copy.wait()
-    pl.semaphore_wait(barrier, count)
+    pl.semaphore_wait(barrier, 7)
 
     sends = []
 
@@ -198,10 +291,12 @@
     theirs = rin[...].astype(F32)
     square = jnp.sum(mine * mine, axis=1, keepdims=True) + jnp.sum(theirs * theirs, axis=1, keepdims=True)
     scaling = lax.rsqrt(square / 2048.0 + EPSILON)
+    gain_v[...] = gain_ref[...].astype(F32)
     for part, at in ((mine, c), (theirs, 1 - c)):
-        lanes = pl.ds(pl.multiple_of(at * 1024, 1024), 1024)
-        gain = gain_ref[:, lanes].astype(F32)
-        tok[0, pl.ds(0, 64), lanes] = (part * scaling * gain).astype(BF16)
+        for i in range(8):
+            lanes = pl.ds(pl.multiple_of(at * 1024 + 128 * i, 128), 128)
+            gain = gain_v[pl.ds(8 * at + i, 1), :]
+            tok[0, pl.ds(0, 64), lanes] = (part[:, 128 * i : 128 * i + 128] * scaling * gain).astype(BF16)
 
     def block(g, l, s, h):
         return tok.at[4 * g + l, pl.ds(64 * s, 64 if g == 0 else ROW_A), pl.ds(1024 * h, 1024)]
@@ -257,8 +352,7 @@
         kind = event[0]
         if kind == "r":
             _, g, l, s, h = event
-            copy = token_copy(g, (l, s), (l, s), h, partner)
-            copy.wait_recv()
+            token_copy(g, (l, s), (l, s), h, partner).wait_recv()
             if s == 0:
                 if l == 0:
                     along_first(g, h, True)
@@ -267,45 +361,40 @@
                     start(token_copy, g, (1, 0), (3, 0), 0, f_next)
                 if (l, h) == (2, 1):
                     start(token_copy, g, (2, 0), (3, 0), 1, f_prev)
-                along_second(g, l, h)
-            if (s, h) == (1, 0):
-                start(token_copy, g, (l, 1), (l, 3), 0, s_next)
-            if (s, h) == (2, 1):
-                start(token_copy, g, (l, 2), (l, 3), 1, s_prev)
-        elif kind == "s":
-            for s in range(4):
-                if (event[1], s) != (0, 0):
-                    start(edge_copy, event[1], s)
-        elif kind == "b":
-            for s in range(4):
-                edge_copy(event[1], s).wait_recv()
+        elif kind == "q":
+            along_second(*event[1:])
+        elif kind == "f":
+            _, g, l, h = event
+            start(token_copy, g, (l, 1 + h), (l, 3), h, s_prev if h else s_next)
+        elif kind == "e":
+            start(edge_copy, event[1], event[2])
+        elif kind == "B":
+            edge_copy(event[1], event[2]).wait_recv()
         elif kind == "w":
-            for i in range(2):
-                weight_copy(event[1], i, 1).wait_recv()
-                start(weight_copy, event[1], i, 2)
-        elif kind == "p":
+            if event[1] == "d":
+                head_copy(1).wait_recv()
+                start(head_copy, 2)
+            else:
+                for i in range(2):
+                    weight_copy(event[1], i, 1).wait_recv()
+                    start(weight_copy, event[1], i, 2)
+        elif event[1] != "d":
             for i in range(2):
                 weight_copy(event[1], i, 2).wait_recv()
         else:
-            head_copy(1).wait_recv()
-            start(head_copy, 2)
             head_copy(0).wait_recv()
             head_copy(2).wait_recv()
             for n in range(4):
                 at, size = WEIGHT_ROWS[n]
-                if n == 0:
-                    for j in range(4):
+                for j in range(4):
+                    if n == 0:
                         heads[3, pl.ds(32 * j, 32)] = folded[j, pl.ds(at, size)]
-                else:
-                    for j in range(4):
+                    else:
                         heads[n - 1 + 4 * (j // 2), pl.ds(64 * (j % 2), 64)] = folded[j, pl.ds(at, size)]
 
-    before_one, before_two = plan()
     for n in range(4):
         for i in range(2):
             weight_copy(n, i, 0).wait_recv()
-    for event in before_one[0]:
-        happen(event)
 
     def unit_one(b):
         product = rows_by(tok[b], wb[0:4].reshape(1024, 2048))
@@ -334,28 +423,28 @@
         slot = g * 16 + (q + 2 * r) * 4 + SEEN_AS[s]
         return remote(src, parts.at[slot], rs_send.at[slot], rs_recv.at[slot], to)
 
-    def step(j, _):
-        for i in range(1, 8):
-
-            @pl.when(j == i)
-            def _():
-                for event in before_one[i]:
-                    happen(event)
-
-        unit_one(j)
-
-        def inner(u, _):
-            for i, events in before_two.items():
+    def step(u, _):
+        for i, (events, _) in enumerate(ORDER):
+            if events:
 
                 @pl.when(u == i)
                 def _():
                     for event in events:
                         happen(event)
 
-            p, k = pick(u, [v[0] for v in UNITS]), pick(u, [v[1] for v in UNITS])
+        wide = pick(u, [int(len(unit) == 1) for _, unit in ORDER])
+        p = pick(u, [unit[0] for _, unit in ORDER])
+        k = pick(u, [unit[-1] for _, unit in ORDER])
+
+        @pl.when(wide == 1)
+        def _():
+            unit_one(p)
+
+        @pl.when(wide == 0)
+        def _():
             total = unit_two(p, k)
 
-            @pl.when(u >= 8)
+            @pl.when(k == 6)
             def _():
                 stage[pl.ds(2 * p, 2)] = total.astype(BF16).reshape(2, 256, 128)
                 for r in range(2):
@@ -369,23 +458,22 @@
                         else:
                             part_copy(p, r, s).start()
 
-            return 0
-
-        low = pick(j, [UNITS_AFTER.get(i, (0, 0))[0] for i in range(8)])
-        high = pick(j, [UNITS_AFTER.get(i, (0, 0))[1] for i in range(8)])
-        lax.fori_loop(low, high, inner, 0)
         return 0
 
-    lax.fori_loop(0, 8, step, 0)
-
-    codes = codes_ref[pl.ds(pl.multiple_of(64 * c, 64), 64), :].astype(F32)
-    ids = ids_ref[pl.ds(pl.multiple_of(64 * c, 64), 64), :]
-    share = codes / (codes[:, 0:1] + codes[:, 1:2])
+    lax.fori_loop(0, len(ORDER), step, 0)
+
+    spot = lax.broadcasted_iota(jnp.int32, (64, 128), 1) == lax.broadcasted_iota(jnp.int32, (64, 128), 0) + 64 * c
+
+    def upright(ref, i):
+        return jnp.sum(jnp.where(spot, ref[i : i + 1, :], 0), axis=1, keepdims=True)
+
+    ids = [upright(ids_ref, i) for i in range(2)]
+    codes = [upright(codes_ref, i).astype(F32) for i in range(2)]
+    share = [code / (codes[0] + codes[1]) for code in codes]
     shares = []
     for j in range(4):
-        named = ids == (z + OFFSET[j]) % 4
-        picked = jnp.where(named, share, 0.0)
-        shares.append(picked[:, 0:1] + picked[:, 1:2])
+        e = (z + OFFSET[j]) % 4
+        shares.append(jnp.where(ids[0] == e, share[0], 0.0) + jnp.where(ids[1] == e, share[1], 0.0))
     c_wide = c.astype(F32)
 
     for slot in range(1, 32):
@@ -397,16 +485,24 @@
             near = parts[slot].astype(F32) if slot else acc[0:64]
             weight = shares[s] * (1.0 - c_wide) + shares[l] * c_wide
             blended += (near + parts[16 + slot].astype(F32)) * weight
-    final[c] = blended
+    rows = pl.ds(pl.multiple_of(64 * c, 64), 64)
+    final_ref[rows] = blended
 
     def final_copy():
-        return remote(final.at[c], final.at[c], fin_sem.at[0], fin_sem.at[1], partner)
+        return remote(final_ref.at[rows], final_ref.at[rows], fin_sem.at[0], fin_sem.at[1], partner)
 
     start(final_copy)
     final_copy().wait_recv()
-    values = final[...].reshape(128, 128)
+
+    for make, args in sends:
+        make(*args).wait_send()
+    for slot in range(1, 32):
+        remote(parts.at[slot], parts.at[slot], rs_send.at[slot], rs_recv.at[slot], partner).wait_send()
+
+
+def last_kernel(final_ref, actions_ref, rewards_ref, trace_ref, values_ref, targets_ref):
+    values = final_ref[...]
     values_ref[...] = values
-
     lane = lax.broadcasted_iota(jnp.int32, (128, 128), 1)
     row = lax.broadcasted_iota(jnp.int32, (128, 128), 0)
 
@@ -426,11 +522,6 @@
     weight = jnp.where(lane >= row, jnp.exp(jnp.minimum(sums_row - sums_column, 0.0)), 0.0)
     target = jnp.sum(weight * driver, axis=1, keepdims=True)
     targets_ref[...] = jnp.sum(jnp.where(lane == row, target, 0.0), axis=0, keepdims=True)
-
-    for make, args in sends:
-        make(*args).wait_send()
-    for slot in range(1, 32):
-        remote(parts.at[slot], parts.at[slot], rs_send.at[slot], rs_recv.at[slot], partner).wait_send()
 
 
 def per_device(
@@ -448,11 +539,11 @@
 ):
     dma = pltpu.SemaphoreType.DMA
     vmem, hbm = pl.BlockSpec(memory_space=pltpu.VMEM), pl.BlockSpec(memory_space=pl.ANY)
-    values, targets = pl.pallas_call(
+    final = pl.pallas_call(
         kernel,
-        out_shape=(jax.ShapeDtypeStruct((128, 128), F32), jax.ShapeDtypeStruct((1, 128), F32)),
-        in_specs=[hbm, vmem, vmem, vmem, hbm, hbm, hbm, hbm, vmem, vmem, vmem],
-        out_specs=(vmem, vmem),
+        out_shape=jax.ShapeDtypeStruct((128, 128), F32),
+        in_specs=[hbm, vmem, vmem, vmem, hbm, hbm, hbm, hbm],
+        out_specs=vmem,
         scratch_shapes=[
             pltpu.VMEM((2, 64, 1024), BF16),
             pltpu.VMEM((64, 1024), BF16),
@@ -465,7 +556,7 @@
             pltpu.VMEM((2048, 128), F32),
             pltpu.VMEM((8, 256, 128), BF16),
             pltpu.VMEM((32, 64, 128), BF16),
-            pltpu.VMEM((2, 64, 128), F32),
+            pltpu.VMEM((16, 128), F32),
             dma((12,)),
             dma((2,)),
             dma((2, 4, 4, 2)),
@@ -486,17 +577,21 @@
         name="critic",
     )(
         tokens,
-        norm_gain.reshape(1, -1),
-        expert_ids,
-        gate_codes,
+        norm_gain.reshape(16, 128),
+        expert_ids.T,
+        gate_codes.T,
         gate_weights,
         up_weights,
         down_weights,
         value_head,
-        actions.reshape(1, -1),
-        rewards.reshape(1, -1),
-        trace_codes.reshape(1, -1),
     )
+    values, targets = pl.pallas_call(
+        last_kernel,
+        out_shape=(jax.ShapeDtypeStruct((128, 128), F32), jax.ShapeDtypeStruct((1, 128), F32)),
+        in_specs=[vmem] * 4,
+        out_specs=(vmem, vmem),
+        name="retrace",
+    )(final, actions.reshape(1, -1), rewards.reshape(1, -1), trace_codes.reshape(1, -1))
     return values, targets.reshape(-1)
 
 

time: 112 us -> 78.5 us (0.70)
  Pallas kernels: 106 us -> 77.7 us
  local copies, waits for them, and re-layouts: 4.83 us -> 0 us
    pallas_call x1 -> x2, Pallas kernels: 106 us -> 77.7 us  [the longest x1 76 us: per_device(): pl.pallas_call(kernel, out_shape=jax.ShapeDtypeStruct((128, 128), F32), i...]
    unnamed x12 -> x0, local copies, waits for them, and re-layouts: 4.23 us -> none
where the time goes in v3:
time: 78.5 us; the launch traced here: 78.4 us
  Pallas kernels  77.7 us (99%)
    pallas_call x1, Pallas kernels, per_device(): pl.pallas_call(kernel, out_shape=jax.ShapeDtypeStruct((128, 128), F32), i...  76 us
    pallas_call x1, Pallas kernels, per_device(): pl.pallas_call(last_kernel, out_shape=(jax.ShapeDtypeStruct((128, 128), F...  1.68 us

profile of v3, /device:TPU:1, one launch (start us, length us, event | category | flops | bytes accessed | tf_op | source)
XLA Modules:
  0.0 78.4 jit_solution(7012176480934037462)
XLA Ops:
  0.6 76.0 %critic.1.final_ref = f32[128,128]{1,0:T(8,128)} custom-call(bf16[128,1024]{1,0:T(8,128)(2,1)} %tokens_ref.1, bf16[16,128]{1,0:T(8,128)(2,1)} %bitcast.7, s32[2,128]{1,0:T(2,128)} %bitcast.8, s32[2,128]{1,0:T(2,128)} %bitcast.9, bf16[1,224,2048]{2,1,0:T(8,128)(2,1)} %gate_ref.1, bf16[1,224,2048]{2,1,0:T(8,128)(2,1)} %up_ref.1, ...), custom_call_target="tpu_custom_call" | custom-call | tf_op jit(solution)/shard_map/critic/pallas_call | solution.py:542
  76.7 1.7 %retrace.1 = (f32[128,128]{1,0:T(8,128)}, f32[1,128]{1,0:T(1,128)}) custom-call(f32[128,128]{1,0:T(8,128)} %critic.1.final_ref, s32[1,128]{1,0:T(1,128)} %bitcast.10, s32[1,128]{1,0:T(1,128)} %bitcast.11, s32[1,128]{1,0:T(1,128)} %bitcast.12), custom_call_target="tpu_custom_call" | custom-call | tf_op jit(solution)/shard_map/retrace/pallas_call | solution.py:588

commit v4 on v3

--- a/solution.py
+++ b/solution.py
@@ -29,133 +29,97 @@
 ORDER = (
     (
         (
-            ("r", 1, 0, 0, 0), ("q", 1, 0, 0), ("r", 0, 1, 0, 0), ("q", 0, 1, 0), ("r", 0, 2, 0, 1),
-            ("r", 0, 0, 1, 0), ("r", 0, 0, 2, 1), ("r", 1, 0, 0, 1), ("f", 0, 0, 0), ("f", 0, 0, 1),
-            ("r", 0, 1, 0, 1), ("e", 1, 0), ("r", 0, 2, 0, 0), ("e", 2, 0), ("r", 0, 0, 1, 1), ("e", 0, 1),
-            ("r", 0, 0, 2, 0), ("e", 0, 2), ("w", 0), ("B", 0, 0), ("w", "d"), ("q", 0, 1, 1), ("p", 0),
-            ("r", 1, 1, 0, 0), ("r", 1, 2, 0, 0), ("r", 1, 0, 1, 0), ("r", 1, 0, 2, 0), ("p", "d"),
-            ("B", 1, 0), ("q", 0, 2, 1), ("B", 2, 0), ("r", 0, 3, 0, 0), ("r", 0, 3, 0, 1), ("e", 3, 0),
-            ("r", 0, 1, 1, 0), ("r", 0, 1, 2, 0), ("B", 0, 1), ("r", 1, 1, 0, 1), ("r", 1, 2, 0, 1),
-            ("q", 0, 2, 0), ("r", 0, 0, 3, 1), ("B", 0, 2), ("r", 0, 0, 3, 0), ("e", 0, 3),
-        ),
-        (0,),
-    ),
-    (
-        (
-            ("f", 0, 1, 0), ("r", 0, 1, 2, 1), ("e", 1, 2), ("f", 0, 1, 1), ("B", 3, 0), ("r", 1, 3, 0, 0),
-            ("r", 0, 1, 1, 1), ("e", 1, 1), ("q", 0, 3, 0), ("B", 0, 3), ("r", 1, 3, 0, 1), ("r", 0, 2, 1, 1),
-            ("r", 0, 2, 2, 1), ("q", 0, 3, 1), ("w", 1), ("B", 1, 2), ("r", 0, 2, 1, 0), ("e", 2, 1),
-            ("r", 0, 2, 2, 0), ("e", 2, 2), ("f", 0, 2, 1), ("f", 0, 2, 0), ("B", 1, 1), ("r", 0, 1, 3, 0),
-            ("r", 0, 1, 3, 1), ("e", 1, 3),
-        ),
-        (1,),
-    ),
-    (
-        (
-            ("q", 1, 0, 1), ("q", 1, 1, 0), ("p", 1), ("r", 0, 3, 1, 0), ("r", 0, 3, 2, 0),
-        ),
-        (0, 4),
+            ("r", 1, 0, 0, 0), ("q", 1, 0, 0), ("w", 0), ("r", 0, 1, 0, 0), ("q", 0, 1, 0), ("r", 0, 2, 0, 1),
+            ("r", 0, 0, 1, 0), ("r", 0, 0, 2, 1), ("f", 0, 0, 0), ("f", 0, 0, 1), ("w", "d"),
+            ("r", 1, 0, 0, 1), ("p", 0), ("p", "d"), ("r", 0, 1, 0, 1), ("e", 1, 0), ("r", 0, 2, 0, 0),
+            ("e", 2, 0), ("r", 0, 0, 1, 1), ("e", 0, 1), ("r", 0, 0, 2, 0), ("e", 0, 2), ("B", 0, 0),
+            ("q", 0, 1, 1), ("r", 1, 1, 0, 0), ("r", 1, 2, 0, 0), ("r", 1, 0, 1, 0), ("r", 1, 0, 2, 0),
+            ("B", 1, 0), ("q", 0, 2, 1), ("r", 0, 3, 0, 0), ("r", 0, 3, 0, 1), ("e", 3, 0), ("r", 0, 1, 1, 0),
+            ("r", 0, 1, 2, 0), ("B", 2, 0), ("B", 0, 1), ("q", 0, 2, 0), ("r", 1, 1, 0, 1), ("r", 1, 2, 0, 1),
+            ("r", 0, 0, 3, 1), ("r", 0, 0, 3, 0), ("e", 0, 3),
+        ),
+        ("A", 0),
+    ),
+    (
+        (
+            ("f", 0, 1, 0), ("B", 0, 2), ("r", 0, 1, 2, 1), ("e", 1, 2), ("f", 0, 1, 1), ("r", 1, 3, 0, 0),
+            ("B", 3, 0), ("q", 0, 3, 0), ("w", 1), ("r", 0, 1, 1, 1), ("e", 1, 1), ("q", 0, 3, 1),
+            ("r", 0, 2, 2, 1), ("r", 0, 2, 1, 1), ("B", 0, 3), ("r", 1, 3, 0, 1), ("p", 1), ("f", 0, 2, 1),
+            ("f", 1, 0, 0), ("r", 0, 2, 1, 0), ("e", 2, 1), ("r", 0, 2, 2, 0), ("e", 2, 2), ("B", 1, 2),
+            ("f", 0, 2, 0), ("r", 0, 1, 3, 0), ("r", 0, 1, 3, 1), ("e", 1, 3),
+        ),
+        ("B", 1),
+    ),
+    (
+        (
+            ("q", 1, 0, 1), ("B", 1, 1), ("r", 0, 3, 1, 0), ("r", 0, 3, 2, 0),
+        ),
+        ("I", 0),
     ),
     (
         (
             ("f", 0, 3, 0), ("B", 2, 1), ("r", 0, 3, 1, 1), ("e", 3, 1), ("r", 0, 3, 2, 1), ("e", 3, 2),
-            ("f", 0, 3, 1), ("B", 2, 2), ("q", 1, 1, 1), ("r", 0, 2, 3, 0), ("r", 0, 2, 3, 1), ("e", 2, 3),
-        ),
-        (2,),
-    ),
-    (
-        (
-            ("f", 1, 0, 0), ("q", 1, 2, 0), ("B", 1, 3), ("r", 1, 0, 1, 1), ("r", 1, 0, 2, 1), ("f", 1, 0, 1),
-            ("B", 3, 1), ("r", 1, 1, 1, 0), ("r", 1, 1, 2, 0), ("q", 1, 2, 1), ("B", 3, 2), ("r", 0, 3, 3, 0),
-            ("r", 0, 3, 3, 1), ("e", 3, 3),
-        ),
-        (3,),
-    ),
-    (
-        (
-            ("f", 1, 1, 0), ("q", 1, 3, 0), ("r", 1, 1, 1, 1), ("r", 1, 1, 2, 1), ("f", 1, 1, 1), ("B", 2, 3),
-        ),
-        (1, 4),
-    ),
-    (
-        (
-            ("q", 1, 3, 1), ("w", 2), ("r", 1, 0, 3, 0), ("r", 1, 2, 2, 0), ("r", 1, 2, 1, 0),
-            ("r", 1, 0, 3, 1),
-        ),
-        (4,),
-    ),
-    (
-        (
-            ("f", 1, 2, 0), ("B", 3, 3), ("r", 1, 2, 1, 1), ("r", 1, 2, 2, 1), ("f", 1, 2, 1), ("p", 2),
-        ),
-        (0, 5),
-    ),
-    (
-        (
-            ("r", 1, 1, 3, 0), ("r", 1, 3, 2, 0),
-        ),
-        (1, 5),
-    ),
-    (
-        (
-            ("r", 1, 3, 1, 0), ("f", 1, 3, 0), ("r", 1, 1, 3, 1),
-        ),
-        (5,),
-    ),
-    (
-        (
-            ("r", 1, 3, 1, 1), ("r", 1, 3, 2, 1), ("f", 1, 3, 1), ("r", 1, 2, 3, 0), ("r", 1, 2, 3, 1),
-        ),
-        (6,),
-    ),
-    (
-        (
-            ("r", 1, 3, 3, 0),
-        ),
-        (2, 4),
-    ),
-    (
-        (
-        ),
-        (2, 5),
-    ),
-    (
-        (
-            ("r", 1, 3, 3, 1),
-        ),
-        (7,),
-    ),
-    (
-        (
-            ("w", 3),
-        ),
-        (3, 4),
-    ),
-    (
-        (
-        ),
-        (3, 5),
+            ("f", 0, 3, 1), ("q", 1, 1, 0), ("B", 2, 2), ("r", 1, 0, 3, 0), ("r", 0, 2, 3, 1), ("q", 1, 1, 1),
+            ("B", 1, 3), ("r", 0, 2, 3, 0), ("e", 2, 3), ("r", 1, 0, 2, 1), ("f", 1, 0, 1),
+        ),
+        ("B", 2),
+    ),
+    (
+        (
+            ("q", 1, 2, 0), ("q", 1, 2, 1), ("r", 1, 0, 1, 1), ("B", 3, 1), ("r", 0, 3, 3, 1), ("w", 2),
+            ("q", 1, 3, 0), ("r", 0, 3, 3, 0), ("e", 3, 3), ("r", 1, 1, 2, 0),
+        ),
+        ("B", 3),
+    ),
+    (
+        (
+            ("q", 1, 3, 1), ("B", 3, 2), ("r", 1, 1, 1, 0), ("r", 1, 1, 2, 1), ("p", 2), ("f", 1, 1, 0),
+            ("f", 1, 1, 1), ("B", 2, 3),
+        ),
+        ("F", 0),
+    ),
+    (
+        (
+            ("r", 1, 1, 1, 1), ("r", 1, 0, 3, 1),
+        ),
+        ("C", 4),
+    ),
+    (
+        (
+            ("r", 1, 2, 1, 0), ("f", 1, 2, 0), ("r", 1, 2, 2, 0), ("B", 3, 3), ("r", 1, 2, 1, 1),
+            ("r", 1, 2, 2, 1), ("f", 1, 2, 1),
+        ),
+        ("F", 1),
+    ),
+    (
+        (
+            ("r", 1, 3, 1, 0), ("f", 1, 3, 0), ("r", 1, 3, 2, 0), ("r", 1, 3, 1, 1), ("r", 1, 3, 2, 1),
+            ("f", 1, 3, 1), ("r", 1, 1, 3, 0), ("r", 1, 1, 3, 1),
+        ),
+        ("C", 5),
+    ),
+    (
+        (
+            ("r", 1, 2, 3, 0), ("r", 1, 2, 3, 1),
+        ),
+        ("C", 6),
+    ),
+    (
+        (
+            ("r", 1, 3, 3, 0), ("r", 1, 3, 3, 1), ("w", 3),
+        ),
+        ("C", 7),
     ),
     (
         (
             ("p", 3),
         ),
-        (0, 6),
-    ),
-    (
-        (
-        ),
-        (1, 6),
-    ),
-    (
-        (
-        ),
-        (2, 6),
-    ),
-    (
-        (
-        ),
-        (3, 6),
+        ("G", 0),
+    ),
+    (
+        (
+        ),
+        ("G", 1),
     ),
 )
 
@@ -396,23 +360,27 @@
         for i in range(2):
             weight_copy(n, i, 0).wait_recv()
 
-    def unit_one(b):
-        product = rows_by(tok[b], wb[0:4].reshape(1024, 2048))
+    def gated(product, count):
         hidden = [
             (silu(product[:, 256 * k : 256 * k + 128]) * product[:, 256 * k + 128 : 256 * k + 256]).astype(BF16)
-            for k in range(4)
+            for k in range(count)
         ]
-        acc[pl.ds(pl.multiple_of(256 * b, 256), 256)] = jnp.dot(
-            jnp.concatenate(hidden, axis=1), heads[0:4].reshape(512, 128), preferred_element_type=F32
-        )
-
-    def unit_two(p, k):
-        product = rows_by(tok[pl.ds(2 * p, 2)].reshape(512, 2048), wb[k])
-        hidden = (silu(product[:, :128]) * product[:, 128:]).astype(BF16)
-        rows = pl.ds(pl.multiple_of(512 * p, 512), 512)
-        total = acc[rows] + jnp.dot(hidden, heads[k], preferred_element_type=F32)
-        acc[rows] = total
-        return total
+        return jnp.concatenate(hidden, axis=1) if count > 1 else hidden[0]
+
+    def unit(b, size, low, high):
+        if high is None:
+            count, weights, head = 1, wb[low], heads[low]
+        else:
+            count = high - low
+            weights = wb[low:high].reshape(256 * count, 2048)
+            head = heads[low:high].reshape(128 * count, 128)
+        product = rows_by(tok[pl.ds(size * b, size)].reshape(256 * size, 2048), weights)
+        value = jnp.dot(gated(product, count), head, preferred_element_type=F32)
+        rows = pl.ds(pl.multiple_of(256 * size * b, 256), 256 * size)
+        if high is not None and low == 0:
+            acc[rows] = value
+        else:
+            acc[rows] += value
 
     def part_copy(p, r, s):
         g, q = p // 2, p % 2
@@ -432,31 +400,41 @@
                     for event in events:
                         happen(event)
 
-        wide = pick(u, [int(len(unit) == 1) for _, unit in ORDER])
-        p = pick(u, [unit[0] for _, unit in ORDER])
-        k = pick(u, [unit[-1] for _, unit in ORDER])
-
-        @pl.when(wide == 1)
+        kind = pick(u, ["ABCDHIEFG".index(work[0]) for _, work in ORDER])
+        b = pick(u, [work[1] for _, work in ORDER])
+        for i, (low, high) in enumerate(((0, 4), (0, 5), (0, 6), (4, 6), (5, 6), (4, 5))):
+
+            @pl.when(kind == i)
+            def _():
+                unit(b, 1, low, high)
+
+        @pl.when((kind == 6) | (kind == 7))
         def _():
-            unit_one(p)
-
-        @pl.when(wide == 0)
+            unit(b, 2, kind - 2, None)
+
+        @pl.when(kind == 8)
         def _():
-            total = unit_two(p, k)
-
-            @pl.when(k == 6)
-            def _():
-                stage[pl.ds(2 * p, 2)] = total.astype(BF16).reshape(2, 256, 128)
+            products = [rows_by(tok[pl.ds(4 * b + 2 * i, 2)].reshape(512, 2048), wb[6]) for i in range(2)]
+            for i in range(2):
+                rows = pl.ds(pl.multiple_of(1024 * b + 512 * i, 512), 512)
+                total = acc[rows] + jnp.dot(gated(products[i], 1), heads[6], preferred_element_type=F32)
+                stage[pl.ds(4 * b + 2 * i, 2)] = total.astype(BF16).reshape(2, 256, 128)
+                if i == 0:
+
+                    @pl.when(b == 0)
+                    def _():
+                        acc[0:64] = total[0:64]
+
                 for r in range(2):
                     for s in range(4):
-                        if (r, s) == (0, 0):
-
-                            @pl.when(p > 0)
+                        if (i, r, s) == (0, 0, 0):
+
+                            @pl.when(b > 0)
                             def _():
-                                part_copy(p, 0, 0).start()
+                                part_copy(2 * b, 0, 0).start()
 
                         else:
-                            part_copy(p, r, s).start()
+                            part_copy(2 * b + i, r, s).start()
 
         return 0
 

time: 78.5 us -> 75.2 us (0.958)
  Pallas kernels: 77.7 us -> 74.3 us
    pallas_call x1, Pallas kernels: 76 us -> 72.6 us  [per_device(): pl.pallas_call(kernel, out_shape=jax.ShapeDtypeStruct((128, 128), F32), i...]
where the time goes in v4:
time: 75.2 us; the launch traced here: 75 us
  Pallas kernels  74.3 us (99%)
    pallas_call x1, Pallas kernels, per_device(): pl.pallas_call(kernel, out_shape=jax.ShapeDtypeStruct((128, 128), F32), i...  72.6 us
    pallas_call x1, Pallas kernels, per_device(): pl.pallas_call(last_kernel, out_shape=(jax.ShapeDtypeStruct((128, 128), F...  1.68 us

profile of v4, /device:TPU:1, one launch (start us, length us, event | category | flops | bytes accessed | tf_op | source)
XLA Modules:
  0.0 75.0 jit_solution(7847856473587777720)
XLA Ops:
  0.6 72.6 %critic.1.final_ref = f32[128,128]{1,0:T(8,128)} custom-call(bf16[128,1024]{1,0:T(8,128)(2,1)} %tokens_ref.1, bf16[16,128]{1,0:T(8,128)(2,1)} %bitcast.7, s32[2,128]{1,0:T(2,128)} %bitcast.8, s32[2,128]{1,0:T(2,128)} %bitcast.9, bf16[1,224,2048]{2,1,0:T(8,128)(2,1)} %gate_ref.1, bf16[1,224,2048]{2,1,0:T(8,128)(2,1)} %up_ref.1, ...), custom_call_target="tpu_custom_call" | custom-call | tf_op jit(solution)/shard_map/critic/pallas_call | solution.py:520
  73.3 1.7 %retrace.1 = (f32[128,128]{1,0:T(8,128)}, f32[1,128]{1,0:T(1,128)}) custom-call(f32[128,128]{1,0:T(8,128)} %critic.1.final_ref, s32[1,128]{1,0:T(1,128)} %bitcast.10, s32[1,128]{1,0:T(1,128)} %bitcast.11, s32[1,128]{1,0:T(1,128)} %bitcast.12), custom_call_target="tpu_custom_call" | custom-call | tf_op jit(solution)/shard_map/retrace/pallas_call | solution.py:566

commit v5 on v4

--- a/solution.py
+++ b/solution.py
@@ -35,54 +35,61 @@
             ("e", 2, 0), ("r", 0, 0, 1, 1), ("e", 0, 1), ("r", 0, 0, 2, 0), ("e", 0, 2), ("B", 0, 0),
             ("q", 0, 1, 1), ("r", 1, 1, 0, 0), ("r", 1, 2, 0, 0), ("r", 1, 0, 1, 0), ("r", 1, 0, 2, 0),
             ("B", 1, 0), ("q", 0, 2, 1), ("r", 0, 3, 0, 0), ("r", 0, 3, 0, 1), ("e", 3, 0), ("r", 0, 1, 1, 0),
-            ("r", 0, 1, 2, 0), ("B", 2, 0), ("B", 0, 1), ("q", 0, 2, 0), ("r", 1, 1, 0, 1), ("r", 1, 2, 0, 1),
-            ("r", 0, 0, 3, 1), ("r", 0, 0, 3, 0), ("e", 0, 3),
+            ("r", 0, 1, 2, 0),
         ),
         ("A", 0),
     ),
     (
         (
-            ("f", 0, 1, 0), ("B", 0, 2), ("r", 0, 1, 2, 1), ("e", 1, 2), ("f", 0, 1, 1), ("r", 1, 3, 0, 0),
-            ("B", 3, 0), ("q", 0, 3, 0), ("w", 1), ("r", 0, 1, 1, 1), ("e", 1, 1), ("q", 0, 3, 1),
-            ("r", 0, 2, 2, 1), ("r", 0, 2, 1, 1), ("B", 0, 3), ("r", 1, 3, 0, 1), ("p", 1), ("f", 0, 2, 1),
-            ("f", 1, 0, 0), ("r", 0, 2, 1, 0), ("e", 2, 1), ("r", 0, 2, 2, 0), ("e", 2, 2), ("B", 1, 2),
-            ("f", 0, 2, 0), ("r", 0, 1, 3, 0), ("r", 0, 1, 3, 1), ("e", 1, 3),
-        ),
-        ("B", 1),
-    ),
-    (
-        (
-            ("q", 1, 0, 1), ("B", 1, 1), ("r", 0, 3, 1, 0), ("r", 0, 3, 2, 0),
-        ),
-        ("I", 0),
-    ),
-    (
-        (
-            ("f", 0, 3, 0), ("B", 2, 1), ("r", 0, 3, 1, 1), ("e", 3, 1), ("r", 0, 3, 2, 1), ("e", 3, 2),
-            ("f", 0, 3, 1), ("q", 1, 1, 0), ("B", 2, 2), ("r", 1, 0, 3, 0), ("r", 0, 2, 3, 1), ("q", 1, 1, 1),
-            ("B", 1, 3), ("r", 0, 2, 3, 0), ("e", 2, 3), ("r", 1, 0, 2, 1), ("f", 1, 0, 1),
+            ("B", 2, 0), ("B", 0, 1), ("q", 0, 2, 0), ("r", 1, 1, 0, 1), ("r", 1, 2, 0, 1), ("r", 0, 0, 3, 1),
+            ("r", 0, 0, 3, 0), ("e", 0, 3), ("B", 0, 2), ("f", 0, 1, 0), ("r", 0, 1, 2, 1), ("e", 1, 2),
+            ("f", 0, 1, 1), ("r", 1, 3, 0, 0), ("B", 3, 0), ("q", 0, 3, 0), ("w", 1), ("r", 0, 1, 1, 1),
+            ("e", 1, 1),
+        ),
+        ("A", 1),
+    ),
+    (
+        (
+            ("q", 0, 3, 1), ("r", 0, 2, 2, 1), ("r", 0, 2, 1, 1), ("B", 0, 3), ("r", 1, 3, 0, 1),
+        ),
+        ("A", 4),
+    ),
+    (
+        (
+            ("f", 0, 2, 1), ("f", 1, 0, 0), ("p", 1), ("r", 0, 2, 1, 0), ("e", 2, 1), ("r", 0, 2, 2, 0),
+            ("e", 2, 2), ("B", 1, 2),
+        ),
+        ("E", 0),
+    ),
+    (
+        (
+            ("f", 0, 2, 0), ("r", 0, 1, 3, 0), ("r", 0, 1, 3, 1), ("e", 1, 3), ("B", 1, 1), ("q", 1, 0, 1),
+            ("r", 0, 3, 1, 0), ("r", 0, 3, 2, 0), ("f", 0, 3, 0), ("B", 2, 1), ("r", 0, 3, 1, 1), ("e", 3, 1),
+            ("r", 0, 3, 2, 1), ("e", 3, 2), ("f", 0, 3, 1),
         ),
         ("B", 2),
     ),
     (
         (
-            ("q", 1, 2, 0), ("q", 1, 2, 1), ("r", 1, 0, 1, 1), ("B", 3, 1), ("r", 0, 3, 3, 1), ("w", 2),
-            ("q", 1, 3, 0), ("r", 0, 3, 3, 0), ("e", 3, 3), ("r", 1, 1, 2, 0),
+            ("q", 1, 1, 0), ("q", 1, 1, 1), ("r", 1, 0, 3, 0), ("B", 2, 2), ("r", 0, 2, 3, 1),
+            ("r", 0, 2, 3, 0), ("e", 2, 3), ("r", 1, 0, 2, 1), ("f", 1, 0, 1), ("B", 1, 3), ("q", 1, 2, 0),
+            ("r", 1, 0, 1, 1), ("q", 1, 2, 1), ("r", 0, 3, 3, 1), ("w", 2), ("B", 3, 1), ("q", 1, 3, 0),
+            ("r", 0, 3, 3, 0), ("e", 3, 3),
         ),
         ("B", 3),
     ),
     (
         (
-            ("q", 1, 3, 1), ("B", 3, 2), ("r", 1, 1, 1, 0), ("r", 1, 1, 2, 1), ("p", 2), ("f", 1, 1, 0),
-            ("f", 1, 1, 1), ("B", 2, 3),
+            ("q", 1, 3, 1), ("r", 1, 1, 2, 0), ("B", 3, 2), ("p", 2), ("r", 1, 1, 1, 0), ("r", 1, 1, 2, 1),
+            ("f", 1, 1, 0),
         ),
         ("F", 0),
     ),
     (
         (
-            ("r", 1, 1, 1, 1), ("r", 1, 0, 3, 1),
-        ),
-        ("C", 4),
+            ("f", 1, 1, 1), ("B", 2, 3), ("r", 1, 1, 1, 1), ("r", 1, 0, 3, 1),
+        ),
+        ("C", 5),
     ),
     (
         (
@@ -93,20 +100,20 @@
     ),
     (
         (
-            ("r", 1, 3, 1, 0), ("f", 1, 3, 0), ("r", 1, 3, 2, 0), ("r", 1, 3, 1, 1), ("r", 1, 3, 2, 1),
-            ("f", 1, 3, 1), ("r", 1, 1, 3, 0), ("r", 1, 1, 3, 1),
-        ),
-        ("C", 5),
-    ),
-    (
-        (
-            ("r", 1, 2, 3, 0), ("r", 1, 2, 3, 1),
+            ("r", 1, 3, 1, 0), ("f", 1, 3, 0), ("r", 1, 3, 2, 0),
+        ),
+        ("D", 4),
+    ),
+    (
+        (
+            ("r", 1, 3, 1, 1), ("r", 1, 3, 2, 1), ("f", 1, 3, 1),
         ),
         ("C", 6),
     ),
     (
         (
-            ("r", 1, 3, 3, 0), ("r", 1, 3, 3, 1), ("w", 3),
+            ("r", 1, 1, 3, 0), ("r", 1, 1, 3, 1), ("r", 1, 2, 3, 0), ("r", 1, 2, 3, 1), ("r", 1, 3, 3, 0),
+            ("r", 1, 3, 3, 1), ("w", 3),
         ),
         ("C", 7),
     ),
@@ -116,12 +123,16 @@
         ),
         ("G", 0),
     ),
-    (
-        (
-        ),
-        ("G", 1),
-    ),
 )
+
+
+BLOCKS = (
+    ((0, 0), (1, 0), (2, 0), (3, 0)),
+    ((0, 1), (0, 2), (1, 1), (1, 2)),
+    ((2, 1), (2, 2), (3, 1), (3, 2)),
+    ((0, 3), (1, 3), (2, 3), (3, 3)),
+)
+PLACE = {block: (i, j) for i, blocks in enumerate(BLOCKS) for j, block in enumerate(blocks)}
 
 
 def pick(index, values):
@@ -133,14 +144,17 @@
 
 def kernel(
     tokens_ref,
-    gain_ref,
-    ids_ref,
-    codes_ref,
+    gain_hbm,
+    ids_hbm,
+    codes_hbm,
     gate_ref,
     up_ref,
     down_ref,
     head_ref,
     final_ref,
+    gain_ref,
+    ids_ref,
+    codes_ref,
     tin,
     rin,
     tok,
@@ -190,6 +204,9 @@
             src_ref=src, dst_ref=dst, send_sem=send, recv_sem=recv, device_id=to, device_id_type=MESH
         )
 
+    barrier = pltpu.get_barrier_semaphore()
+    for to in (partner, other, twin, f_next, f_prev, s_next, s_prev):
+        pl.semaphore_signal(barrier, inc=1, device_id=to, device_id_type=MESH)
     loads = [pltpu.make_async_copy(tokens_ref.at[pl.ds(i * 64, 64)], tin.at[i], local_sem.at[i]) for i in range(2)]
     w_loads = []
     for n, (at, size) in enumerate(WEIGHT_ROWS):
@@ -204,12 +221,13 @@
         pltpu.make_async_copy(down_ref.at[0], down_v, local_sem.at[10]),
         pltpu.make_async_copy(head_ref, head_v, local_sem.at[11]),
     ]
-    for copy in loads + w_loads + d_loads:
+    small = [
+        pltpu.make_async_copy(src, dst, local_sem.at[12 + i])
+        for i, (src, dst) in enumerate(((gain_hbm, gain_ref), (ids_hbm, ids_ref), (codes_hbm, codes_ref)))
+    ]
+    for copy in loads + w_loads[:2] + small[:1] + w_loads[2:] + d_loads + small[1:]:
         copy.start()
 
-    barrier = pltpu.get_barrier_semaphore()
-    for to in (partner, other, twin, f_next, f_prev, s_next, s_prev):
-        pl.semaphore_signal(barrier, inc=1, device_id=to, device_id_type=MESH)
     for copy in loads:
         copy.wait()
     pl.semaphore_wait(barrier, 7)
@@ -224,7 +242,7 @@
         return remote(tin.at[1 - c], rin, raw_sem.at[0], raw_sem.at[1], partner)
 
     start(raw_copy)
-    for copy in w_loads:
+    for copy in w_loads[:2]:
         copy.wait()
 
     def weight_copy(n, i, role):
@@ -246,6 +264,10 @@
 
     for i in range(2):
         start(weight_copy, 0, i, 1)
+    for copy in small:
+        copy.wait()
+    for copy in w_loads[2:]:
+        copy.wait()
     for n in range(4):
         for i in range(2):
             start(weight_copy, n, i, 0)
@@ -263,7 +285,8 @@
             tok[0, pl.ds(0, 64), lanes] = (part[:, 128 * i : 128 * i + 128] * scaling * gain).astype(BF16)
 
     def block(g, l, s, h):
-        return tok.at[4 * g + l, pl.ds(64 * s, 64 if g == 0 else ROW_A), pl.ds(1024 * h, 1024)]
+        i, j = PLACE[l, s]
+        return tok.at[4 * g + i, pl.ds(64 * j, 64 if g == 0 else ROW_A), pl.ds(1024 * h, 1024)]
 
     def token_copy(g, src, dst, h, to):
         return remote(
@@ -280,11 +303,12 @@
         else:
             start(token_copy, g, (0, 0), (2, 0), h, f_prev)
 
-    def edge(ref, l, s):
-        return ref.at[l, pl.ds(64 * s + ROW_A, 64 - ROW_A)]
+    def edge(g, l, s):
+        i, j = PLACE[l, s]
+        return tok.at[4 * g + i, pl.ds(64 * j + ROW_A, 64 - ROW_A)]
 
     def edge_copy(l, s):
-        return remote(edge(tok, l, s), edge(tok, 4 + l, s), b_send.at[l, s], b_recv.at[l, s], twin)
+        return remote(edge(0, l, s), edge(1, l, s), b_send.at[l, s], b_recv.at[l, s], twin)
 
     def twin_copy(h):
         src = tok.at[0, pl.ds(0, ROW_A), pl.ds(1024 * h, 1024)]
@@ -382,17 +406,27 @@
         else:
             acc[rows] += value
 
-    def part_copy(p, r, s):
-        g, q = p // 2, p % 2
-        to = device(
-            x + g * (x_two - x), (first + q + r * (3 - 2 * q)) % 4, (second + OFFSET[s]) % 4
+    def part_copy(g, l, s):
+        to = device(x_two if g else x, (first + OFFSET[l]) % 4, (second + OFFSET[s]) % 4)
+        i, j = PLACE[l, s]
+        slot = 16 * g + 4 * SEEN_AS[l] + SEEN_AS[s]
+        return remote(
+            stage.at[4 * g + i, pl.ds(64 * j, 64)], parts.at[slot], rs_send.at[slot], rs_recv.at[slot], to
         )
-        src = stage.at[2 * p + r, pl.ds(64 * s, 64)]
-        slot = g * 16 + (q + 2 * r) * 4 + SEEN_AS[s]
-        return remote(src, parts.at[slot], rs_send.at[slot], rs_recv.at[slot], to)
+
+    def finish(p, product):
+        rows = pl.ds(512 * p, 512)
+        total = acc[rows] + jnp.dot(gated(product, 1), heads[6], preferred_element_type=F32)
+        stage[pl.ds(2 * p, 2)] = total.astype(BF16).reshape(2, 256, 128)
+        for i in (2 * p + 1, 2 * p):
+            for l, s in BLOCKS[i % 4]:
+                if (i // 4, l, s) != (0, 0, 0):
+                    part_copy(i // 4, l, s).start()
+        if p == 0:
+            acc[0:64] = total[0:64]
 
     def step(u, _):
-        for i, (events, _) in enumerate(ORDER):
+        for i, (events, _) in enumerate(ORDER[:-1]):
             if events:
 
                 @pl.when(u == i)
@@ -400,8 +434,8 @@
                     for event in events:
                         happen(event)
 
-        kind = pick(u, ["ABCDHIEFG".index(work[0]) for _, work in ORDER])
-        b = pick(u, [work[1] for _, work in ORDER])
+        kind = pick(u, ["ABCDHIEFG".index(work[0]) for _, work in ORDER[:-1]])
+        b = pick(u, [work[1] for _, work in ORDER[:-1]])
         for i, (low, high) in enumerate(((0, 4), (0, 5), (0, 6), (4, 6), (5, 6), (4, 5))):
 
             @pl.when(kind == i)
@@ -412,33 +446,19 @@
         def _():
             unit(b, 2, kind - 2, None)
 
-        @pl.when(kind == 8)
-        def _():
-            products = [rows_by(tok[pl.ds(4 * b + 2 * i, 2)].reshape(512, 2048), wb[6]) for i in range(2)]
-            for i in range(2):
-                rows = pl.ds(pl.multiple_of(1024 * b + 512 * i, 512), 512)
-                total = acc[rows] + jnp.dot(gated(products[i], 1), heads[6], preferred_element_type=F32)
-                stage[pl.ds(4 * b + 2 * i, 2)] = total.astype(BF16).reshape(2, 256, 128)
-                if i == 0:
-
-                    @pl.when(b == 0)
-                    def _():
-                        acc[0:64] = total[0:64]
-
-                for r in range(2):
-                    for s in range(4):
-                        if (i, r, s) == (0, 0, 0):
-
-                            @pl.when(b > 0)
-                            def _():
-                                part_copy(2 * b, 0, 0).start()
-
-                        else:
-                            part_copy(2 * b + i, r, s).start()
-
         return 0
 
-    lax.fori_loop(0, len(ORDER), step, 0)
+    lax.fori_loop(0, len(ORDER) - 1, step, 0)
+
+    for event in ORDER[-1][0]:
+        happen(event)
+    product = None
+    for p in (3, 2, 1, 0):
+        ahead = rows_by(tok[2 * p : 2 * p + 2].reshape(512, 2048), wb[6])
+        if p < 3:
+            finish(p + 1, product)
+        product = ahead
+    finish(0, product)
 
     spot = lax.broadcasted_iota(jnp.int32, (64, 128), 1) == lax.broadcasted_iota(jnp.int32, (64, 128), 0) + 64 * c
 
@@ -454,15 +474,18 @@
         shares.append(jnp.where(ids[0] == e, share[0], 0.0) + jnp.where(ids[1] == e, share[1], 0.0))
     c_wide = c.astype(F32)
 
-    for slot in range(1, 32):
+    def arrived(slot):
         remote(parts.at[slot], parts.at[slot], rs_send.at[slot], rs_recv.at[slot], partner).wait_recv()
+        return parts[slot].astype(F32)
+
     blended = jnp.zeros((64, 128), F32)
-    for l in range(4):
-        for s in range(4):
+    for s in (3, 2, 1, 0):
+        for l in (3, 2, 1, 0):
             slot = 4 * l + s
-            near = parts[slot].astype(F32) if slot else acc[0:64]
             weight = shares[s] * (1.0 - c_wide) + shares[l] * c_wide
-            blended += (near + parts[16 + slot].astype(F32)) * weight
+            far = arrived(16 + slot)
+            near = arrived(slot) if slot else acc[0:64]
+            blended += (near + far) * weight
     rows = pl.ds(pl.multiple_of(64 * c, 64), 64)
     final_ref[rows] = blended
 
@@ -519,10 +542,13 @@
     vmem, hbm = pl.BlockSpec(memory_space=pltpu.VMEM), pl.BlockSpec(memory_space=pl.ANY)
     final = pl.pallas_call(
         kernel,
-        out_shape=jax.ShapeDtypeStruct((128, 128), F32),
-        in_specs=[hbm, vmem, vmem, vmem, hbm, hbm, hbm, hbm],
+        out_shape=pltpu.VMEM((128, 128), F32),
+        in_specs=[hbm] * 8,
         out_specs=vmem,
         scratch_shapes=[
+            pltpu.VMEM((16, 128), BF16),
+            pltpu.VMEM((2, 128), jnp.int32),
+            pltpu.VMEM((2, 128), jnp.int32),
             pltpu.VMEM((2, 64, 1024), BF16),
             pltpu.VMEM((64, 1024), BF16),
             pltpu.VMEM((8, 256, 2048), BF16),
@@ -535,7 +561,7 @@
             pltpu.VMEM((8, 256, 128), BF16),
             pltpu.VMEM((32, 64, 128), BF16),
             pltpu.VMEM((16, 128), F32),
-            dma((12,)),
+            dma((15,)),
             dma((2,)),
             dma((2, 4, 4, 2)),
             dma((2, 4, 4, 2)),
@@ -569,7 +595,7 @@
         in_specs=[vmem] * 4,
         out_specs=(vmem, vmem),
         name="retrace",
-    )(final, actions.reshape(1, -1), rewards.reshape(1, -1), trace_codes.reshape(1, -1))
+    )(pltpu.with_memory_space_constraint(final, pltpu.VMEM), actions.reshape(1, -1), rewards.reshape(1, -1), trace_codes.reshape(1, -1))
     return values, targets.reshape(-1)
 
 

time: 75.2 us -> 71.4 us (0.949)
  Pallas kernels: 74.3 us -> 70.6 us
    pallas_call x1, Pallas kernels: 72.6 us -> 69.1 us  [per_device(): pl.pallas_call(kernel, out_shape=pltpu.VMEM((128, 128), F32), in_specs=[h...]
where the time goes in v5:
time: 71.4 us; the launch traced here: 71.3 us
  Pallas kernels  70.6 us (99%)
    pallas_call x1, Pallas kernels, per_device(): pl.pallas_call(kernel, out_shape=pltpu.VMEM((128, 128), F32), in_specs=[h...  69.1 us
    pallas_call x1, Pallas kernels, per_device(): pl.pallas_call(last_kernel, out_shape=(jax.ShapeDtypeStruct((128, 128), F...  1.51 us

profile of v5, /device:TPU:1, one launch (start us, length us, event | category | flops | bytes accessed | tf_op | source)
XLA Modules:
  0.0 71.3 jit_solution(5286204007279510770)
XLA Ops:
  0.6 69.1 %critic.1.final_ref = f32[128,128]{1,0:T(8,128)S(1)} custom-call(bf16[128,1024]{1,0:T(8,128)(2,1)} %tokens_ref.1, bf16[16,128]{1,0:T(8,128)(2,1)} %bitcast.7, s32[2,128]{1,0:T(2,128)} %bitcast.8, s32[2,128]{1,0:T(2,128)} %bitcast.9, bf16[1,224,2048]{2,1,0:T(8,128)(2,1)} %gate_ref.1, bf16[1,224,2048]{2,1,0:T(8,128)(2,1)} %up_ref.1, ...), custom_call_target="tpu_custom_call" | custom-call | tf_op jit(solution)/shard_map/critic/pallas_call | solution.py:543
  69.8 1.5 %retrace.1 = (f32[128,128]{1,0:T(8,128)}, f32[1,128]{1,0:T(1,128)}) custom-call(f32[128,128]{1,0:T(8,128)S(1)} %critic.1.final_ref, s32[1,128]{1,0:T(1,128)} %bitcast.10, s32[1,128]{1,0:T(1,128)} %bitcast.11, s32[1,128]{1,0:T(1,128)} %bitcast.12), custom_call_target="tpu_custom_call" | custom-call | tf_op jit(solution)/shard_map/retrace/pallas_call | solution.py:592

commit v6 on v5

--- a/solution.py
+++ b/solution.py
@@ -29,91 +29,89 @@
 ORDER = (
     (
         (
-            ("r", 1, 0, 0, 0), ("q", 1, 0, 0), ("w", 0), ("r", 0, 1, 0, 0), ("q", 0, 1, 0), ("r", 0, 2, 0, 1),
-            ("r", 0, 0, 1, 0), ("r", 0, 0, 2, 1), ("f", 0, 0, 0), ("f", 0, 0, 1), ("w", "d"),
-            ("r", 1, 0, 0, 1), ("p", 0), ("p", "d"), ("r", 0, 1, 0, 1), ("e", 1, 0), ("r", 0, 2, 0, 0),
-            ("e", 2, 0), ("r", 0, 0, 1, 1), ("e", 0, 1), ("r", 0, 0, 2, 0), ("e", 0, 2), ("B", 0, 0),
-            ("q", 0, 1, 1), ("r", 1, 1, 0, 0), ("r", 1, 2, 0, 0), ("r", 1, 0, 1, 0), ("r", 1, 0, 2, 0),
-            ("B", 1, 0), ("q", 0, 2, 1), ("r", 0, 3, 0, 0), ("r", 0, 3, 0, 1), ("e", 3, 0), ("r", 0, 1, 1, 0),
+            ("r", 1, 0, 0, 0), ("q", 1, 0, 0), ("r", 0, 1, 0, 0), ("q", 0, 1, 0), ("r", 0, 2, 0, 1),
+            ("r", 0, 0, 1, 0), ("r", 0, 0, 2, 1), ("f", 0, 0, 0), ("f", 0, 0, 1), ("w", 0), ("r", 1, 0, 0, 1),
+            ("w", "d"), ("p", 0), ("r", 0, 1, 0, 1), ("e", 1, 0), ("r", 0, 2, 0, 0), ("e", 2, 0),
+            ("r", 0, 0, 1, 1), ("e", 0, 1), ("r", 0, 0, 2, 0), ("e", 0, 2), ("B", 0, 0), ("q", 0, 1, 1),
+            ("p", "d"), ("r", 1, 1, 0, 0), ("r", 1, 2, 0, 0), ("r", 1, 0, 1, 0), ("r", 1, 0, 2, 0),
+            ("q", 0, 2, 1), ("B", 1, 0), ("r", 0, 3, 0, 0), ("r", 0, 3, 0, 1), ("e", 3, 0), ("r", 0, 1, 1, 0),
             ("r", 0, 1, 2, 0),
         ),
         ("A", 0),
     ),
     (
         (
-            ("B", 2, 0), ("B", 0, 1), ("q", 0, 2, 0), ("r", 1, 1, 0, 1), ("r", 1, 2, 0, 1), ("r", 0, 0, 3, 1),
-            ("r", 0, 0, 3, 0), ("e", 0, 3), ("B", 0, 2), ("f", 0, 1, 0), ("r", 0, 1, 2, 1), ("e", 1, 2),
-            ("f", 0, 1, 1), ("r", 1, 3, 0, 0), ("B", 3, 0), ("q", 0, 3, 0), ("w", 1), ("r", 0, 1, 1, 1),
-            ("e", 1, 1),
+            ("f", 0, 1, 0), ("B", 2, 0), ("r", 1, 1, 0, 1), ("r", 1, 2, 0, 1), ("q", 0, 2, 0),
+            ("r", 0, 0, 3, 1), ("B", 0, 1), ("r", 0, 0, 3, 0), ("e", 0, 3), ("q", 0, 3, 0), ("r", 0, 1, 2, 1),
+            ("e", 1, 2), ("f", 0, 1, 1), ("B", 0, 2), ("r", 1, 3, 0, 0), ("r", 0, 1, 1, 1), ("e", 1, 1),
         ),
         ("A", 1),
     ),
     (
         (
-            ("q", 0, 3, 1), ("r", 0, 2, 2, 1), ("r", 0, 2, 1, 1), ("B", 0, 3), ("r", 1, 3, 0, 1),
+            ("q", 0, 3, 1), ("r", 0, 2, 2, 1), ("B", 3, 0), ("w", 1), ("r", 0, 2, 1, 1), ("f", 0, 2, 1),
+            ("f", 1, 0, 0), ("r", 1, 3, 0, 1),
         ),
         ("A", 4),
     ),
     (
         (
-            ("f", 0, 2, 1), ("f", 1, 0, 0), ("p", 1), ("r", 0, 2, 1, 0), ("e", 2, 1), ("r", 0, 2, 2, 0),
-            ("e", 2, 2), ("B", 1, 2),
+            ("q", 1, 0, 1), ("B", 0, 3), ("r", 0, 1, 3, 0), ("r", 0, 2, 2, 0), ("e", 2, 2), ("p", 1),
         ),
         ("E", 0),
     ),
     (
         (
-            ("f", 0, 2, 0), ("r", 0, 1, 3, 0), ("r", 0, 1, 3, 1), ("e", 1, 3), ("B", 1, 1), ("q", 1, 0, 1),
-            ("r", 0, 3, 1, 0), ("r", 0, 3, 2, 0), ("f", 0, 3, 0), ("B", 2, 1), ("r", 0, 3, 1, 1), ("e", 3, 1),
-            ("r", 0, 3, 2, 1), ("e", 3, 2), ("f", 0, 3, 1),
+            ("q", 1, 1, 0), ("B", 1, 2), ("r", 0, 2, 1, 0), ("e", 2, 1), ("f", 0, 2, 0), ("r", 0, 3, 2, 0),
+            ("B", 1, 1), ("r", 0, 3, 1, 0), ("r", 0, 1, 3, 1), ("e", 1, 3), ("f", 0, 3, 0), ("r", 0, 3, 1, 1),
+            ("e", 3, 1), ("r", 0, 3, 2, 1), ("e", 3, 2), ("f", 0, 3, 1),
         ),
         ("B", 2),
     ),
     (
         (
-            ("q", 1, 1, 0), ("q", 1, 1, 1), ("r", 1, 0, 3, 0), ("B", 2, 2), ("r", 0, 2, 3, 1),
-            ("r", 0, 2, 3, 0), ("e", 2, 3), ("r", 1, 0, 2, 1), ("f", 1, 0, 1), ("B", 1, 3), ("q", 1, 2, 0),
-            ("r", 1, 0, 1, 1), ("q", 1, 2, 1), ("r", 0, 3, 3, 1), ("w", 2), ("B", 3, 1), ("q", 1, 3, 0),
-            ("r", 0, 3, 3, 0), ("e", 3, 3),
+            ("q", 1, 1, 1), ("q", 1, 2, 0), ("r", 1, 0, 3, 0), ("r", 0, 2, 3, 1), ("B", 2, 2),
+            ("r", 1, 0, 1, 1), ("r", 1, 0, 2, 1), ("f", 1, 0, 1), ("q", 1, 2, 1), ("B", 2, 1),
+            ("r", 1, 1, 1, 0), ("r", 1, 1, 2, 0), ("f", 1, 1, 0), ("B", 1, 3), ("r", 0, 2, 3, 0), ("e", 2, 3),
+            ("q", 1, 3, 0), ("w", 2), ("r", 0, 3, 3, 1), ("q", 1, 3, 1), ("B", 3, 1), ("r", 0, 3, 3, 0),
+            ("e", 3, 3),
         ),
         ("B", 3),
     ),
     (
         (
-            ("q", 1, 3, 1), ("r", 1, 1, 2, 0), ("B", 3, 2), ("p", 2), ("r", 1, 1, 1, 0), ("r", 1, 1, 2, 1),
-            ("f", 1, 1, 0),
+            ("r", 1, 1, 2, 1), ("f", 1, 1, 1), ("p", 2), ("r", 1, 1, 1, 1), ("B", 3, 2), ("r", 1, 2, 2, 0),
+        ),
+        ("C", 5),
+    ),
+    (
+        (
+            ("r", 1, 2, 1, 0), ("f", 1, 2, 0), ("r", 1, 0, 3, 1), ("r", 1, 2, 1, 1), ("B", 2, 3),
+            ("r", 1, 2, 2, 1), ("f", 1, 2, 1),
         ),
         ("F", 0),
     ),
     (
         (
-            ("f", 1, 1, 1), ("B", 2, 3), ("r", 1, 1, 1, 1), ("r", 1, 0, 3, 1),
-        ),
-        ("C", 5),
-    ),
-    (
-        (
-            ("r", 1, 2, 1, 0), ("f", 1, 2, 0), ("r", 1, 2, 2, 0), ("B", 3, 3), ("r", 1, 2, 1, 1),
-            ("r", 1, 2, 2, 1), ("f", 1, 2, 1),
+            ("r", 1, 1, 3, 0), ("r", 1, 3, 2, 0), ("B", 3, 3),
         ),
         ("F", 1),
     ),
     (
         (
-            ("r", 1, 3, 1, 0), ("f", 1, 3, 0), ("r", 1, 3, 2, 0),
+            ("r", 1, 3, 1, 0), ("f", 1, 3, 0), ("r", 1, 3, 2, 1), ("f", 1, 3, 1),
         ),
         ("D", 4),
     ),
     (
         (
-            ("r", 1, 3, 1, 1), ("r", 1, 3, 2, 1), ("f", 1, 3, 1),
+            ("r", 1, 3, 1, 1), ("r", 1, 1, 3, 1),
         ),
         ("C", 6),
     ),
     (
         (
-            ("r", 1, 1, 3, 0), ("r", 1, 1, 3, 1), ("r", 1, 2, 3, 0), ("r", 1, 2, 3, 1), ("r", 1, 3, 3, 0),
-            ("r", 1, 3, 3, 1), ("w", 3),
+            ("r", 1, 2, 3, 0), ("r", 1, 2, 3, 1), ("w", 3), ("r", 1, 3, 3, 0), ("r", 1, 3, 3, 1),
         ),
         ("C", 7),
     ),
@@ -124,7 +122,6 @@
         ("G", 0),
     ),
 )
-
 
 BLOCKS = (
     ((0, 0), (1, 0), (2, 0), (3, 0)),

time: 71.4 us -> 69.5 us (0.973)
  Pallas kernels: 70.6 us -> 68.7 us
    pallas_call x1, Pallas kernels: 69.1 us -> 67.2 us  [per_device(): pl.pallas_call(kernel, out_shape=pltpu.VMEM((128, 128), F32), in_specs=[h...]
where the time goes in v6:
time: 69.5 us; the launch traced here: 69.3 us
  Pallas kernels  68.7 us (99%)
    pallas_call x1, Pallas kernels, per_device(): pl.pallas_call(kernel, out_shape=pltpu.VMEM((128, 128), F32), in_specs=[h...  67.2 us
    pallas_call x1, Pallas kernels, per_device(): pl.pallas_call(last_kernel, out_shape=(jax.ShapeDtypeStruct((128, 128), F...  1.51 us

profile of v6, /device:TPU:1, one launch (start us, length us, event | category | flops | bytes accessed | tf_op | source)
XLA Modules:
  0.0 69.3 jit_solution(11877305306070656279)
XLA Ops:
  0.6 67.2 %critic.1.final_ref = f32[128,128]{1,0:T(8,128)S(1)} custom-call(bf16[128,1024]{1,0:T(8,128)(2,1)} %tokens_ref.1, bf16[16,128]{1,0:T(8,128)(2,1)} %bitcast.7, s32[2,128]{1,0:T(2,128)} %bitcast.8, s32[2,128]{1,0:T(2,128)} %bitcast.9, bf16[1,224,2048]{2,1,0:T(8,128)(2,1)} %gate_ref.1, bf16[1,224,2048]{2,1,0:T(8,128)(2,1)} %up_ref.1, ...), custom_call_target="tpu_custom_call" | custom-call | tf_op jit(solution)/shard_map/critic/pallas_call | solution.py:540
  67.8 1.5 %retrace.1 = (f32[128,128]{1,0:T(8,128)}, f32[1,128]{1,0:T(1,128)}) custom-call(f32[128,128]{1,0:T(8,128)S(1)} %critic.1.final_ref, s32[1,128]{1,0:T(1,128)} %bitcast.10, s32[1,128]{1,0:T(1,128)} %bitcast.11, s32[1,128]{1,0:T(1,128)} %bitcast.12), custom_call_target="tpu_custom_call" | custom-call | tf_op jit(solution)/shard_map/retrace/pallas_call | solution.py:589

commit v7 on v6

--- a/solution.py
+++ b/solution.py
@@ -29,89 +29,89 @@
 ORDER = (
     (
         (
-            ("r", 1, 0, 0, 0), ("q", 1, 0, 0), ("r", 0, 1, 0, 0), ("q", 0, 1, 0), ("r", 0, 2, 0, 1),
-            ("r", 0, 0, 1, 0), ("r", 0, 0, 2, 1), ("f", 0, 0, 0), ("f", 0, 0, 1), ("w", 0), ("r", 1, 0, 0, 1),
-            ("w", "d"), ("p", 0), ("r", 0, 1, 0, 1), ("e", 1, 0), ("r", 0, 2, 0, 0), ("e", 2, 0),
-            ("r", 0, 0, 1, 1), ("e", 0, 1), ("r", 0, 0, 2, 0), ("e", 0, 2), ("B", 0, 0), ("q", 0, 1, 1),
-            ("p", "d"), ("r", 1, 1, 0, 0), ("r", 1, 2, 0, 0), ("r", 1, 0, 1, 0), ("r", 1, 0, 2, 0),
-            ("q", 0, 2, 1), ("B", 1, 0), ("r", 0, 3, 0, 0), ("r", 0, 3, 0, 1), ("e", 3, 0), ("r", 0, 1, 1, 0),
+            ("r", 1, 0, 0, 0), ("q", 1, 0, 0), ("w", 0), ("r", 0, 1, 0, 0), ("q", 0, 1, 0), ("r", 0, 2, 0, 1),
+            ("q", 0, 2, 1), ("r", 0, 0, 1, 0), ("r", 0, 0, 2, 1), ("w", "d"), ("r", 1, 0, 0, 1), ("p", 0),
+            ("f", 0, 0, 0), ("f", 0, 0, 1), ("p", "d"), ("r", 0, 1, 0, 1), ("e", 1, 0), ("r", 0, 2, 0, 0),
+            ("e", 2, 0), ("r", 0, 0, 1, 1), ("e", 0, 1), ("r", 0, 0, 2, 0), ("e", 0, 2), ("B", 0, 0),
+            ("q", 0, 1, 1), ("r", 1, 1, 0, 0), ("r", 1, 2, 0, 0), ("r", 1, 0, 1, 0), ("r", 1, 0, 2, 0),
+            ("q", 0, 2, 0), ("B", 1, 0), ("r", 0, 3, 0, 0), ("r", 0, 3, 0, 1), ("e", 3, 0), ("r", 0, 1, 1, 0),
             ("r", 0, 1, 2, 0),
         ),
         ("A", 0),
     ),
     (
         (
-            ("f", 0, 1, 0), ("B", 2, 0), ("r", 1, 1, 0, 1), ("r", 1, 2, 0, 1), ("q", 0, 2, 0),
-            ("r", 0, 0, 3, 1), ("B", 0, 1), ("r", 0, 0, 3, 0), ("e", 0, 3), ("q", 0, 3, 0), ("r", 0, 1, 2, 1),
-            ("e", 1, 2), ("f", 0, 1, 1), ("B", 0, 2), ("r", 1, 3, 0, 0), ("r", 0, 1, 1, 1), ("e", 1, 1),
+            ("B", 2, 0), ("f", 0, 1, 0), ("r", 1, 1, 0, 1), ("r", 1, 2, 0, 1), ("r", 0, 2, 2, 1),
+            ("f", 0, 2, 1), ("B", 0, 1), ("r", 0, 2, 1, 1), ("q", 0, 3, 0), ("r", 0, 0, 3, 1), ("B", 0, 2),
+            ("r", 1, 3, 0, 0), ("q", 0, 3, 1), ("w", 1), ("r", 0, 0, 3, 0), ("e", 0, 3), ("r", 0, 1, 2, 1),
+            ("e", 1, 2), ("B", 3, 0), ("f", 0, 1, 1), ("f", 1, 0, 0), ("r", 0, 1, 1, 1), ("e", 1, 1),
         ),
         ("A", 1),
     ),
     (
         (
-            ("q", 0, 3, 1), ("r", 0, 2, 2, 1), ("B", 3, 0), ("w", 1), ("r", 0, 2, 1, 1), ("f", 0, 2, 1),
-            ("f", 1, 0, 0), ("r", 1, 3, 0, 1),
-        ),
-        ("A", 4),
-    ),
-    (
-        (
-            ("q", 1, 0, 1), ("B", 0, 3), ("r", 0, 1, 3, 0), ("r", 0, 2, 2, 0), ("e", 2, 2), ("p", 1),
+            ("q", 1, 0, 1), ("p", 1), ("r", 1, 3, 0, 1), ("r", 0, 2, 1, 0), ("e", 2, 1), ("r", 0, 2, 2, 0),
+            ("e", 2, 2),
+        ),
+        ("B", 4),
+    ),
+    (
+        (
+            ("f", 0, 2, 0), ("q", 1, 1, 0), ("r", 0, 1, 3, 0), ("r", 0, 2, 3, 1), ("B", 0, 3),
         ),
         ("E", 0),
     ),
     (
         (
-            ("q", 1, 1, 0), ("B", 1, 2), ("r", 0, 2, 1, 0), ("e", 2, 1), ("f", 0, 2, 0), ("r", 0, 3, 2, 0),
-            ("B", 1, 1), ("r", 0, 3, 1, 0), ("r", 0, 1, 3, 1), ("e", 1, 3), ("f", 0, 3, 0), ("r", 0, 3, 1, 1),
-            ("e", 3, 1), ("r", 0, 3, 2, 1), ("e", 3, 2), ("f", 0, 3, 1),
+            ("q", 1, 1, 1), ("r", 0, 3, 1, 0), ("r", 0, 3, 2, 0), ("B", 1, 2), ("f", 0, 3, 0),
+            ("r", 0, 3, 1, 1), ("e", 3, 1), ("r", 0, 3, 2, 1), ("e", 3, 2), ("f", 0, 3, 1),
         ),
         ("B", 2),
     ),
     (
         (
-            ("q", 1, 1, 1), ("q", 1, 2, 0), ("r", 1, 0, 3, 0), ("r", 0, 2, 3, 1), ("B", 2, 2),
-            ("r", 1, 0, 1, 1), ("r", 1, 0, 2, 1), ("f", 1, 0, 1), ("q", 1, 2, 1), ("B", 2, 1),
-            ("r", 1, 1, 1, 0), ("r", 1, 1, 2, 0), ("f", 1, 1, 0), ("B", 1, 3), ("r", 0, 2, 3, 0), ("e", 2, 3),
-            ("q", 1, 3, 0), ("w", 2), ("r", 0, 3, 3, 1), ("q", 1, 3, 1), ("B", 3, 1), ("r", 0, 3, 3, 0),
-            ("e", 3, 3),
-        ),
-        ("B", 3),
-    ),
-    (
-        (
-            ("r", 1, 1, 2, 1), ("f", 1, 1, 1), ("p", 2), ("r", 1, 1, 1, 1), ("B", 3, 2), ("r", 1, 2, 2, 0),
-        ),
-        ("C", 5),
-    ),
-    (
-        (
-            ("r", 1, 2, 1, 0), ("f", 1, 2, 0), ("r", 1, 0, 3, 1), ("r", 1, 2, 1, 1), ("B", 2, 3),
-            ("r", 1, 2, 2, 1), ("f", 1, 2, 1),
+            ("q", 1, 2, 0), ("B", 1, 1), ("r", 1, 0, 3, 0), ("r", 0, 1, 3, 1), ("e", 1, 3), ("B", 2, 1),
+            ("q", 1, 2, 1), ("r", 1, 0, 1, 1), ("r", 1, 0, 2, 1), ("f", 1, 0, 1), ("q", 1, 3, 0), ("B", 2, 2),
+            ("r", 0, 2, 3, 0), ("e", 2, 3), ("r", 1, 1, 2, 0), ("w", 2), ("q", 1, 3, 1), ("r", 1, 1, 1, 0),
+            ("r", 1, 1, 2, 1), ("B", 3, 1), ("f", 1, 1, 0), ("f", 1, 1, 1), ("r", 1, 1, 1, 1),
+        ),
+        ("B", 5),
+    ),
+    (
+        (
+            ("p", 2), ("r", 0, 3, 3, 1), ("B", 3, 2), ("r", 0, 3, 3, 0), ("e", 3, 3), ("r", 1, 2, 2, 0),
+            ("B", 1, 3),
+        ),
+        ("C", 3),
+    ),
+    (
+        (
+            ("r", 1, 2, 1, 0), ("f", 1, 2, 0), ("r", 1, 2, 2, 1), ("f", 1, 2, 1), ("B", 2, 3),
+            ("r", 1, 2, 1, 1), ("r", 1, 0, 3, 1),
         ),
         ("F", 0),
     ),
     (
         (
-            ("r", 1, 1, 3, 0), ("r", 1, 3, 2, 0), ("B", 3, 3),
-        ),
-        ("F", 1),
-    ),
-    (
-        (
-            ("r", 1, 3, 1, 0), ("f", 1, 3, 0), ("r", 1, 3, 2, 1), ("f", 1, 3, 1),
-        ),
-        ("D", 4),
-    ),
-    (
-        (
-            ("r", 1, 3, 1, 1), ("r", 1, 1, 3, 1),
+            ("r", 1, 3, 1, 0), ("f", 1, 3, 0), ("r", 1, 3, 2, 0),
+        ),
+        ("F", 2),
+    ),
+    (
+        (
+            ("r", 1, 3, 1, 1), ("r", 1, 3, 2, 1), ("f", 1, 3, 1),
         ),
         ("C", 6),
     ),
     (
         (
-            ("r", 1, 2, 3, 0), ("r", 1, 2, 3, 1), ("w", 3), ("r", 1, 3, 3, 0), ("r", 1, 3, 3, 1),
+            ("B", 3, 3), ("r", 1, 1, 3, 0), ("r", 1, 1, 3, 1), ("r", 1, 2, 3, 0), ("r", 1, 2, 3, 1),
+        ),
+        ("H", 2),
+    ),
+    (
+        (
+            ("w", 3), ("r", 1, 3, 3, 0), ("r", 1, 3, 3, 1),
         ),
         ("C", 7),
     ),
@@ -475,6 +475,8 @@
         remote(parts.at[slot], parts.at[slot], rs_send.at[slot], rs_recv.at[slot], partner).wait_recv()
         return parts[slot].astype(F32)
 
+    for make, args in sends:
+        make(*args).wait_send()
     blended = jnp.zeros((64, 128), F32)
     for s in (3, 2, 1, 0):
         for l in (3, 2, 1, 0):
@@ -489,13 +491,11 @@
     def final_copy():
         return remote(final_ref.at[rows], final_ref.at[rows], fin_sem.at[0], fin_sem.at[1], partner)
 
-    start(final_copy)
-    final_copy().wait_recv()
-
-    for make, args in sends:
-        make(*args).wait_send()
+    final_copy().start()
     for slot in range(1, 32):
         remote(parts.at[slot], parts.at[slot], rs_send.at[slot], rs_recv.at[slot], partner).wait_send()
+    final_copy().wait_recv()
+    final_copy().wait_send()
 
 
 def last_kernel(final_ref, actions_ref, rewards_ref, trace_ref, values_ref, targets_ref):

time: 69.5 us -> 68.9 us (level)
  no operation moved by 1% of the time
where the time goes in v7:
time: 68.9 us; the launch traced here: 68.8 us
  Pallas kernels  68.2 us (99%)
    pallas_call x1, Pallas kernels, per_device(): pl.pallas_call(kernel, out_shape=pltpu.VMEM((128, 128), F32), in_specs=[h...  66.6 us
    pallas_call x1, Pallas kernels, per_device(): pl.pallas_call(last_kernel, out_shape=(jax.ShapeDtypeStruct((128, 128), F...  1.51 us

profile of v7, /device:TPU:1, one launch (start us, length us, event | category | flops | bytes accessed | tf_op | source)
XLA Modules:
  0.0 68.8 jit_solution(18345532324052302149)
XLA Ops:
  0.6 66.6 %critic.1.final_ref = f32[128,128]{1,0:T(8,128)S(1)} custom-call(bf16[128,1024]{1,0:T(8,128)(2,1)} %tokens_ref.1, bf16[16,128]{1,0:T(8,128)(2,1)} %bitcast.7, s32[2,128]{1,0:T(2,128)} %bitcast.8, s32[2,128]{1,0:T(2,128)} %bitcast.9, bf16[1,224,2048]{2,1,0:T(8,128)(2,1)} %gate_ref.1, bf16[1,224,2048]{2,1,0:T(8,128)(2,1)} %up_ref.1, ...), custom_call_target="tpu_custom_call" | custom-call | tf_op jit(solution)/shard_map/critic/pallas_call | solution.py:540
  67.3 1.5 %retrace.1 = (f32[128,128]{1,0:T(8,128)}, f32[1,128]{1,0:T(1,128)}) custom-call(f32[128,128]{1,0:T(8,128)S(1)} %critic.1.final_ref, s32[1,128]{1,0:T(1,128)} %bitcast.10, s32[1,128]{1,0:T(1,128)} %bitcast.11, s32[1,128]{1,0:T(1,128)} %bitcast.12), custom_call_target="tpu_custom_call" | custom-call | tf_op jit(solution)/shard_map/retrace/pallas_call | solution.py:589
